TPU v7x, 32 devices: a 4x4x1 block of a 4x4x8 slice. The times are simulated.
32 devices in a mesh: dp: 1 (over z), fsdp: 32 (over y, x, core).
Axes of the slice: x: 4, y: 4, z: 1, core: 2. Of those that a mesh axis runs over, the one named last changes fastest.
The devices are a block of a 4x4x8 slice.
Arguments:
- x: bfloat16 [32, 64, 2048], P(('dp', 'fsdp'))
- gain: bfloat16 [2, 2048], replicated
- w_in: bfloat16 [2, 2048, 18944], P(None, None, 'fsdp')
- w_out: bfloat16 [2, 10240, 2048], P(None, 'fsdp')
Outputs:
- output 1: bfloat16 [32, 64, 2048], P(('dp', 'fsdp'))
- output 2: bfloat16 [2, 32, 64, 256], P(None, ('dp', 'fsdp'))
- output 3: bfloat16 [2, 32, 64, 256], P(None, ('dp', 'fsdp'))
All inputs are finite; a program needn't handle non-finite values.
Results may differ from a plain program's by a relative error of at most 0.0128833.
Values are sent between devices in bfloat16 or wider.
A program may use at most 768 MiB of HBM per device.

v0:
```python
import jax
import jax.numpy as jnp
from jax import lax
from jax.sharding import PartitionSpec as P

HEAD_DIM = 256
ROPE_BASE = 10000.0
NORM_EPS = 1e-6


def layer_norm(hidden, gain_vec):
    x_float = hidden.astype(jnp.float32)
    centred = x_float - jnp.mean(x_float, axis=-1, keepdims=True)
    variance = jnp.mean(centred * centred, axis=-1, keepdims=True)
    return (centred * lax.rsqrt(variance + NORM_EPS) * gain_vec.astype(jnp.float32)).astype(jnp.bfloat16)


def rope_tables(seq_len):
    half_dim = HEAD_DIM // 2
    inv_freq = ROPE_BASE ** (-jnp.arange(half_dim, dtype=jnp.float32) / half_dim)
    angle = jnp.arange(seq_len, dtype=jnp.float32)[:, None] * inv_freq[None, :]
    return jnp.cos(angle), jnp.sin(angle)


def apply_rope(tensor, cos_table, sin_table):
    half_dim = HEAD_DIM // 2
    first = tensor[..., :half_dim]
    second = tensor[..., half_dim:]
    return jnp.concatenate([first * cos_table - second * sin_table, second * cos_table + first * sin_table], axis=-1)


def mix_tokens(projected, num_heads, ff_dim):
    batch, seq_len, _ = projected.shape
    q_cols = num_heads * HEAD_DIM
    query = projected[..., :q_cols].reshape(batch, seq_len, num_heads, HEAD_DIM)
    key_raw = projected[..., q_cols:q_cols + HEAD_DIM]
    value = projected[..., q_cols + HEAD_DIM:q_cols + 2 * HEAD_DIM]
    gate = projected[..., q_cols + 2 * HEAD_DIM:q_cols + 2 * HEAD_DIM + ff_dim]
    up_proj = projected[..., q_cols + 2 * HEAD_DIM + ff_dim:]
    cos_table, sin_table = rope_tables(seq_len)
    q_rot = (apply_rope(query.astype(jnp.float32), cos_table[:, None, :], sin_table[:, None, :]) * HEAD_DIM ** -0.5).astype(jnp.bfloat16)
    k_rot = apply_rope(key_raw.astype(jnp.float32), cos_table, sin_table).astype(jnp.bfloat16)
    scores = jnp.einsum("crie,cle->cril", q_rot, k_rot, preferred_element_type=jnp.float32)
    causal = jnp.arange(seq_len)[:, None, None] >= jnp.arange(seq_len)[None, None, :]
    scores = jnp.where(causal, scores, -1e30)
    exp_scores = jnp.exp(scores - jnp.max(scores, axis=-1, keepdims=True))
    row_sum = jnp.sum(exp_scores, axis=-1, keepdims=True)
    attended = jnp.einsum("cril,cle->crie", exp_scores.astype(jnp.bfloat16), value, preferred_element_type=jnp.float32) / row_sum
    attended = attended.astype(jnp.bfloat16).reshape(batch, seq_len, q_cols)
    gated = (jax.nn.silu(gate.astype(jnp.float32)) * up_proj.astype(jnp.float32)).astype(jnp.bfloat16)
    return attended, gated, k_rot, value


def parallel_layer(hidden, gain_vec, w_in_full, w_out_full):
    out_rows = w_out_full.shape[0]
    ff_dim = w_in_full.shape[1] - out_rows - 2 * HEAD_DIM
    num_heads = (out_rows - ff_dim) // HEAD_DIM
    q_cols = num_heads * HEAD_DIM
    normed = layer_norm(hidden, gain_vec)
    projected = jnp.einsum("bsd,de->bse", normed, w_in_full, preferred_element_type=jnp.float32).astype(jnp.bfloat16)
    attended, gated, k_rot, value = mix_tokens(projected, num_heads, ff_dim)
    out_sum = jnp.einsum("bsr,rd->bsd", attended, w_out_full[:q_cols], preferred_element_type=jnp.float32)
    out_sum = out_sum + jnp.einsum("bsf,fd->bsd", gated, w_out_full[q_cols:], preferred_element_type=jnp.float32)
    new_hidden = (hidden.astype(jnp.float32) + out_sum).astype(jnp.bfloat16)
    return new_hidden, k_rot, value


def solution(mesh):
    batch_axes = ("dp", "fsdp")

    def device_program(x_local, gain, w_in_local, w_out_local):
        hidden = x_local
        key_list = []
        value_list = []
        for layer in range(w_in_local.shape[0]):
            w_in_full = lax.all_gather(w_in_local[layer], "fsdp", axis=1, tiled=True)
            w_out_full = lax.all_gather(w_out_local[layer], "fsdp", axis=0, tiled=True)
            hidden, k_rot, value = parallel_layer(hidden, gain[layer], w_in_full, w_out_full)
            key_list.append(k_rot)
            value_list.append(value)
        return hidden, jnp.stack(key_list), jnp.stack(value_list)

    return jax.shard_map(
        device_program,
        mesh=mesh,
        in_specs=(P(batch_axes, None, None), P(None, None), P(None, None, "fsdp"), P(None, "fsdp", None)),
        out_specs=(P(batch_axes, None, None), P(None, batch_axes, None, None), P(None, batch_axes, None, None)),
        check_vma=False,
    )
```

profile of v0, /device:TPU:96, one launch (start us, length us, event | category | flops | bytes accessed | tf_op | source)
XLA Modules:
  0.0 751.8 jit_solution(18025242762968219065)
XLA Ops:
  7.3 5.5 fusion.94
  12.9 1.7 fusion.95
  14.8 0.7 all-gather.13.cloned.1.call-update
  15.5 0.6 all-gather.15.cloned.1.call-update
  16.2 0.1 convert_reduce_fusion
  16.3 0.2 fusion.47
  16.6 0.1 fusion.83
  16.7 221.9 %all-gather.9.cloned.1.call-done = bf16[1,2048,18944]{1,2,0:T(8,128)(2,1)} async-done(((bf16[1,2048,592]{1,2,0:T(8,128)(2,1)}), bf16[1,2048,18944]{1,2,0:T(8,128)(2,1)}) %all-gather.9.cloned.1.call-update) | async-done | bytes 77594640 | tf_op jit(solution)/shard_map/all_gather | solution.py:76
  238.7 30.9 %fusion.15 = bf16[1,64,18944]{2,1,0:T(8,128)(2,1)S(1)} fusion(bf16[1,2048,18944]{1,2,0:T(8,128)(2,1)} %all-gather.9.cloned.1.call-done, bf16[1,64,2048]{2,1,0:T(8,128)(2,1)S(1)} %copy-done.1, f32[2048]{0:T(1024)S(1)} %bitcast.135, f32[64]{0:T(128)S(1)} %add_rsqrt_fusion.1, f32[64]{0:T(128)S(1)} %broadcast_multiply_fusion.1), kind=kOutput, calls=%fused_computation.11 | convolution fusion | flops 4967923712 | bytes 80290304 | tf_op jit(solution)/shard_map/bsd,de->bse/dot_general | solution.py:60
  269.6 0.2 copy.7
  269.8 0.6 slice_bitcast_fusion.27
  270.4 0.2 subtract_convert_fusion.1
  270.6 0.1 subtract_bitcast_fusion.1
  270.7 0.3 fusion.96
  271.0 0.2 copy-done.2
  271.2 0.2 fusion.66
  271.4 0.3 fusion.39
  271.8 98.3 %all-gather.11.cloned.1.call-done = bf16[1,10240,2048]{2,1,0:T(8,128)(2,1)} async-done(((bf16[1,320,2048]{2,1,0:T(8,128)(2,1)}), bf16[1,10240,2048]{2,1,0:T(8,128)(2,1)}) %all-gather.11.cloned.1.call-update) | async-done | bytes 41943056 | tf_op jit(solution)/shard_map/all_gather | solution.py:77
  370.1 13.7 %fusion.5 = f32[64,2048]{1,0:T(8,128)} fusion(bf16[1,10240,2048]{2,1,0:T(8,128)(2,1)} %all-gather.11.cloned.1.call-done, bf16[1,64,18944]{2,1,0:T(8,128)(2,1)S(1)} %fusion.15), kind=kOutput, calls=%fused_computation.7 | convolution fusion | flops 2151677952 | bytes 36175872 | tf_op jit(solution)/shard_map/bsf,fd->bsd/dot_general | solution.py:63
  383.8 5.1 fusion.97
  389.0 0.2 multiply_reduce_fusion
  389.2 205.3 %all-gather.13.cloned.1.call-done = bf16[1,2048,18944]{1,2,0:T(8,128)(2,1)} async-done(((bf16[1,2048,592]{1,2,0:T(8,128)(2,1)}), bf16[1,2048,18944]{1,2,0:T(8,128)(2,1)}) %all-gather.13.cloned.1.call-update) | async-done | bytes 77594640 | tf_op jit(solution)/shard_map/all_gather | solution.py:76
  594.5 31.5 %fusion.12 = bf16[1,64,18944]{2,1,0:T(8,128)(2,1)S(1)} fusion(bf16[1,2048,18944]{1,2,0:T(8,128)(2,1)} %all-gather.13.cloned.1.call-done, f32[1,64,2048]{2,1,0:T(8,128)S(1)} %get-tuple-element.26, f32[2048]{0:T(1024)S(1)} %bitcast.134, f32[64]{0:T(128)S(1)} %add_rsqrt_fusion, f32[64]{0:T(128)S(1)} %broadcast_multiply_fusion), kind=kOutput, calls=%fused_computation.10 | convolution fusion | flops 4967792640 | bytes 80552448 | tf_op jit(solution)/shard_map/bsd,de->bse/dot_general | solution.py:60
  626.0 0.2 copy.9
  626.2 0.2 subtract_convert_fusion
  626.5 0.3 fusion.98
  626.8 0.2 fusion.68
  627.0 0.3 fusion.40
  627.4 0.7 maximum_maximum_fusion
  628.1 97.8 %all-gather.15.cloned.1.call-done = bf16[1,10240,2048]{2,1,0:T(8,128)(2,1)} async-done(((bf16[1,320,2048]{2,1,0:T(8,128)(2,1)}), bf16[1,10240,2048]{2,1,0:T(8,128)(2,1)}) %all-gather.15.cloned.1.call-update) | async-done | bytes 41943056 | tf_op jit(solution)/shard_map/all_gather | solution.py:77
  725.8 13.7 %fusion.4 = f32[64,2048]{1,0:T(8,128)} fusion(bf16[1,10240,2048]{2,1,0:T(8,128)(2,1)} %all-gather.15.cloned.1.call-done, bf16[1,64,18944]{2,1,0:T(8,128)(2,1)S(1)} %fusion.12), kind=kOutput, calls=%fused_computation.5 | convolution fusion | flops 2151677952 | bytes 36175872 | tf_op jit(solution)/shard_map/bsf,fd->bsd/dot_general | solution.py:63
  739.5 5.8 fusion.26
  (38 shorter events, 0.7 us)
Async XLA Ops:
  7.2 231.5 %all-gather.9.cloned.1.call-start = ((), (), s32[]{:S(2)}) async-start(), calls=%async_computation | async-start | bytes 80019456 | tf_op jit(solution)/shard_map/all_gather | solution.py:76
  7.2 5.7 copy-start
  12.9 357.2 %all-gather.11.cloned.1.call-start = ((), (), s32[]{:S(2)}) async-start(), calls=%async_computation.1 | async-start | bytes 43253760 | tf_op jit(solution)/shard_map/all_gather | solution.py:77
  14.6 1.6 copy-start.1
  14.7 2.0 copy-start.7
  14.7 579.8 %all-gather.13.cloned.1.call-start = ((), (), s32[]{:S(2)}) async-start(), calls=%async_computation.2 | async-start | bytes 80019456 | tf_op jit(solution)/shard_map/all_gather | solution.py:76
  15.5 710.3 %all-gather.15.cloned.1.call-start = ((), (), s32[]{:S(2)}) async-start(), calls=%async_computation.3 | async-start | bytes 43253760 | tf_op jit(solution)/shard_map/all_gather | solution.py:77
  16.1 254.3 %copy-start.8 = (f32[128]{0:T(128)}, f32[128]{0:T(128)S(1)}, u32[]{:S(2)}) copy-start(f32[128]{0:T(128)S(1)} %multiply_power_fusion) | copy-start | bytes 1540
  270.6 0.6 copy-start.2
  270.6 0.6 copy-start.4
  594.5 31.7 %copy-start.9 = (f32[128]{0:T(128)S(1)}, f32[128]{0:T(128)}, u32[]{:S(2)}) copy-start(f32[128]{0:T(128)} %copy-done.8) | copy-start | bytes 1540
  626.4 1.0 copy-start.3
  626.4 1.0 copy-start.5
  626.4 1.0 copy-start.6
Sparse Core Ops, SparseCore 0:
  13.0 225.6 all-gather.8
  240.7 129.3 all-gather.10
  372.2 222.2 all-gather.12
  596.4 129.3 all-gather.14
where the time goes:
time: 754 us; the launch traced here: 752 us
  waiting for transfers between devices  625 us (83%)
  matrix products  102 us (14%)
  between operations  14 us (2%)
  local copies, waits for them, and re-layouts  7.9 us (1%)
    all_gather x2, waiting for transfers between devices, device_program(): w_in_full = lax.all_gather(w_in_local[layer], 'fsdp', axis=1, tiled=True)  427 us
    all_gather x2, waiting for transfers between devices, device_program(): w_out_full = lax.all_gather(w_out_local[layer], 'fsdp', axis=0, tiled=True)  196 us
    dot_general x2, matrix products, parallel_layer(): jnp.einsum('bsd,de->bse', normed, w_in_full, preferred_element_type=jnp.f...  62.4 us
    dot_general x2, matrix products, parallel_layer(): jnp.einsum('bsf,fd->bsd', gated, w_out_full[q_cols:], preferred_element_t...  27.4 us
  transfers between devices with their start and end apart: 4, of which 4 were waited for; matrix products, arithmetic and copies ran while one was open for 12% of the time, Pallas kernels for 0%

commit v1 on v0

--- a/solution.py
+++ b/solution.py
@@ -51,17 +51,25 @@
     return attended, gated, k_rot, value
 
 
-def parallel_layer(hidden, gain_vec, w_in_full, w_out_full):
-    out_rows = w_out_full.shape[0]
-    ff_dim = w_in_full.shape[1] - out_rows - 2 * HEAD_DIM
+def parallel_layer(hidden, gain_vec, w_in_part, w_out_part, group):
+    batch, seq_len, d_model = hidden.shape
+    in_part = w_in_part.shape[1]
+    out_part = w_out_part.shape[0]
+    out_rows = out_part * group
+    ff_dim = in_part * group - out_rows - 2 * HEAD_DIM
     num_heads = (out_rows - ff_dim) // HEAD_DIM
-    q_cols = num_heads * HEAD_DIM
-    normed = layer_norm(hidden, gain_vec)
-    projected = jnp.einsum("bsd,de->bse", normed, w_in_full, preferred_element_type=jnp.float32).astype(jnp.bfloat16)
+    tokens = batch * seq_len
+    normed = layer_norm(hidden, gain_vec).reshape(tokens, d_model)
+    normed_all = lax.all_gather(normed, "fsdp", axis=0, tiled=True)
+    projected = jnp.dot(normed_all, w_in_part, preferred_element_type=jnp.float32).astype(jnp.bfloat16)
+    projected = lax.all_to_all(projected.reshape(group, tokens, in_part), "fsdp", 0, 0, tiled=True)
+    projected = jnp.transpose(projected, (1, 0, 2)).reshape(batch, seq_len, group * in_part)
     attended, gated, k_rot, value = mix_tokens(projected, num_heads, ff_dim)
-    out_sum = jnp.einsum("bsr,rd->bsd", attended, w_out_full[:q_cols], preferred_element_type=jnp.float32)
-    out_sum = out_sum + jnp.einsum("bsf,fd->bsd", gated, w_out_full[q_cols:], preferred_element_type=jnp.float32)
-    new_hidden = (hidden.astype(jnp.float32) + out_sum).astype(jnp.bfloat16)
+    mixed = jnp.concatenate([attended, gated], axis=-1).reshape(tokens, group, out_part)
+    mixed = lax.all_to_all(jnp.transpose(mixed, (1, 0, 2)), "fsdp", 0, 0, tiled=True)
+    partial = jnp.dot(mixed.reshape(group * tokens, out_part), w_out_part, preferred_element_type=jnp.float32)
+    out_sum = lax.psum_scatter(partial, "fsdp", scatter_dimension=0, tiled=True)
+    new_hidden = (hidden.astype(jnp.float32) + out_sum.reshape(hidden.shape)).astype(jnp.bfloat16)
     return new_hidden, k_rot, value
 
 
@@ -73,9 +81,7 @@
         key_list = []
         value_list = []
         for layer in range(w_in_local.shape[0]):
-            w_in_full = lax.all_gather(w_in_local[layer], "fsdp", axis=1, tiled=True)
-            w_out_full = lax.all_gather(w_out_local[layer], "fsdp", axis=0, tiled=True)
-            hidden, k_rot, value = parallel_layer(hidden, gain[layer], w_in_full, w_out_full)
+            hidden, k_rot, value = parallel_layer(hidden, gain[layer], w_in_local[layer], w_out_local[layer], mesh.shape["fsdp"])
             key_list.append(k_rot)
             value_list.append(value)
         return hidden, jnp.stack(key_list), jnp.stack(value_list)

time: 754 us -> 537 us (0.71)
  waiting for transfers between devices: 625 us -> 342 us
  blocking collectives: 0 us -> 93.8 us
  matrix products: 102 us -> 37.5 us
  local copies, waits for them, and re-layouts: 7.9 us -> 26.5 us
  other arithmetic: 3.09 us -> 17.7 us
    all_gather x4 -> x2, waiting for transfers between devices: 623 us -> 96.9 us  [parallel_layer(): normed_all = lax.all_gather(normed, 'fsdp', axis=0, tiled=True)]
    reduce_scatter x0 -> x2, waiting for transfers between devices: none -> 210 us  [parallel_layer(): out_sum = lax.psum_scatter(partial, 'fsdp', scatter_dimension=0, tiled=True)]
    all_to_all x0 -> x3, blocking collectives: none -> 93.8 us  [the longest x2 55.2 us: parallel_layer(): lax.all_to_all(jnp.transpose(mixed, (1, 0, 2)), 'fsdp', 0, 0, tiled=True)]
    dot_general x6 -> x4, matrix products: 101 us -> 35.6 us  [the longest x2 19.5 us: parallel_layer(): jnp.dot(normed_all, w_in_part, preferred_element_type=jnp.float32)]
    all_to_all x0 -> x1, waiting for transfers between devices: none -> 34.6 us  [parallel_layer(): lax.all_to_all(projected.reshape(group, tokens, in_part), 'fsdp', 0, 0, t...]
    reshape x0 -> x8, local copies, waits for them, and re-layouts: none -> 16 us  [the longest x2 10.9 us: parallel_layer(): jnp.transpose(projected, (1, 0, 2)).reshape(batch, seq_len, group * in_part)]
    convert_element_type x0 -> x5, other arithmetic: none -> 8.21 us  [the longest x2 3.76 us: mix_tokens(): (jax.nn.silu(gate.astype(jnp.float32)) * up_proj.astype(jnp.float32)).ast...]
  transfers between devices with their start and end apart: 4 -> 5, of which waited for: 4 -> 5; matrix products, arithmetic and copies ran while one was open for 12% -> 0% of each run, Pallas kernels for 0% -> 0%
where the time goes in v1:
time: 537 us; the launch traced here: 536 us
  waiting for transfers between devices  342 us (64%)
  blocking collectives  93.8 us (17%)
  matrix products  37.5 us (7%)
  local copies, waits for them, and re-layouts  26.5 us (5%)
  other arithmetic  17.7 us (3%)
  between operations  14 us (3%)
    reduce_scatter x2, waiting for transfers between devices, parallel_layer(): out_sum = lax.psum_scatter(partial, 'fsdp', scatter_dimension=0, tiled=True)  210 us
    all_gather x2, waiting for transfers between devices, parallel_layer(): normed_all = lax.all_gather(normed, 'fsdp', axis=0, tiled=True)  96.9 us
    all_to_all x2, blocking collectives, parallel_layer(): lax.all_to_all(jnp.transpose(mixed, (1, 0, 2)), 'fsdp', 0, 0, tiled=True)  55.2 us
    all_to_all x1, blocking collectives, parallel_layer(): lax.all_to_all(projected.reshape(group, tokens, in_part), 'fsdp', 0, 0, t...  38.7 us
    all_to_all x1, waiting for transfers between devices, parallel_layer(): lax.all_to_all(projected.reshape(group, tokens, in_part), 'fsdp', 0, 0, t...  34.6 us
    dot_general x2, matrix products, parallel_layer(): jnp.dot(normed_all, w_in_part, preferred_element_type=jnp.float32)  19.5 us
    dot_general x2, matrix products, parallel_layer(): jnp.dot(mixed.reshape(group * tokens, out_part), w_out_part, preferred_el...  16.2 us
    reshape x2, local copies, waits for them, and re-layouts, parallel_layer(): jnp.transpose(projected, (1, 0, 2)).reshape(batch, seq_len, group * in_part)  10.9 us
  transfers between devices with their start and end apart: 5, of which 5 were waited for; matrix products, arithmetic and copies ran while one was open for 0% of the time, Pallas kernels for 0%

profile of v1, /device:TPU:96, one launch (start us, length us, event | category | flops | bytes accessed | tf_op | source)
XLA Modules:
  0.0 536.4 jit_solution(8662206390206440127)
XLA Ops:
  7.2 1.1 convert_reduce_fusion.1
  8.3 1.2 fusion.39
  10.4 1.8 fusion.41
  12.2 50.0 %all-gather.5.cloned.1.call-done = bf16[1,2048,2048]{2,1,0:T(8,128)(2,1)} async-done(((bf16[1,64,2048]{2,1,0:T(8,128)(2,1)}), bf16[1,2048,2048]{2,1,0:T(8,128)(2,1)}) %all-gather.5.cloned.1.call-update) | async-done | bytes 8388624 | tf_op jit(solution)/shard_map/all_gather | solution.py:63
  62.2 9.2 %fusion.4 = bf16[2048,592]{0,1:T(8,128)(2,1)S(1)} fusion(bf16[1,2048,2048]{2,1,0:T(8,128)(2,1)} %all-gather.5.cloned.1.call-done, bf16[2,2048,592]{1,2,0:T(8,128)(2,1)} %param.6), kind=kOutput, calls=%fused_computation.4 | convolution fusion | flops 4967268352 | bytes 13238272 | tf_op jit(solution)/shard_map/dot_general | solution.py:64
  71.5 2.6 copy.9
  74.0 4.9 all-to-all-start
  79.2 34.6 %all-to-all-done = bf16[32,64,592]{2,1,0:T(8,128)(2,1)S(1)} async-done(((bf16[32,64,592]{2,1,0:T(8,128)(2,1)}), bf16[32,64,592]{2,1,0:T(8,128)(2,1)S(1)}, u32[]{:S(2)}, u32[]{:S(2)}) %all-to-all-start) | async-done | bytes 2424864 | tf_op jit(solution)/shard_map/all_to_all | solution.py:65
  113.8 3.0 copy.10
  116.8 5.5 %reshape.431 = bf16[1,64,18944]{2,1,0:T(8,128)(2,1)S(1)} reshape(bf16[64,32,592]{2,1,0:T(8,128)(2,1)} %copy.10) | data formatting | bytes 4849664 | tf_op jit(solution)/shard_map/reshape | solution.py:66
  122.3 1.6 fusion.23
  125.3 1.3 pad_maximum_fusion
  126.6 1.9 reshape.434
  129.0 27.6 %all_to_all.20 = bf16[32,64,320]{2,1,0:T(8,128)(2,1)S(1)} all-to-all(bf16[32,64,320]{2,1,0:T(8,128)(2,1)S(1)} %bitcast.95), channel_id=1, replica_groups=mesh['dp'=1,'fsdp'=32] {'fsdp'}, dimensions={0} | all-to-all | bytes 2621440 | tf_op jit(solution)/shard_map/all_to_all | solution.py:69
  156.6 8.1 %fusion.26 = f32[2048,2048]{1,0:T(8,128)} fusion(bf16[2048,320]{1,0:T(8,128)(2,1)S(1)} %bitcast.93, bf16[2,320,2048]{2,1,0:T(8,128)(2,1)S(1)} %copy-done.1), kind=kOutput, calls=%fused_computation.30 | convolution fusion | flops 2684354560 | bytes 19660800 | tf_op jit(solution)/shard_map/dot_general | solution.py:70
  164.9 105.1 %reduce-scatter.3.cloned.1.call-done = f32[64,2048]{1,0:T(8,128)} async-done(((f32[2048,2048]{1,0:T(8,128)}), f32[64,2048]{1,0:T(8,128)}) %reduce-scatter.3.cloned.1.call-update) | async-done | bytes 524304 | tf_op jit(solution)/shard_map/reduce_scatter | solution.py:71
  270.0 1.2 convert_reduce_fusion
  271.5 0.9 fusion.38
  272.5 46.9 %all-gather.7.cloned.1.call-done = bf16[1,2048,2048]{2,1,0:T(8,128)(2,1)} async-done(((bf16[1,64,2048]{2,1,0:T(8,128)(2,1)}), bf16[1,2048,2048]{2,1,0:T(8,128)(2,1)}) %all-gather.7.cloned.1.call-update) | async-done | bytes 8388624 | tf_op jit(solution)/shard_map/all_gather | solution.py:63
  319.3 10.2 %fusion.7 = bf16[2048,592]{0,1:T(8,128)(2,1)} fusion(bf16[1,2048,2048]{2,1,0:T(8,128)(2,1)} %all-gather.7.cloned.1.call-done, bf16[2,2048,592]{1,2,0:T(8,128)(2,1)} %param.6), kind=kOutput, calls=%fused_computation.5 | convolution fusion | flops 4967268352 | bytes 13238272 | tf_op jit(solution)/shard_map/dot_general | solution.py:64
  329.6 3.1 copy.12
  332.7 38.7 %all_to_all.21 = bf16[32,64,592]{2,1,0:T(8,128)(2,1)S(1)} all-to-all(bf16[32,64,592]{2,1,0:T(8,128)(2,1)S(1)} %bitcast.91), channel_id=1, replica_groups=mesh['dp'=1,'fsdp'=32] {'fsdp'}, dimensions={0} | all-to-all | bytes 4849664 | tf_op jit(solution)/shard_map/all_to_all | solution.py:65
  371.3 1.5 copy.13
  372.8 5.4 %reshape.439 = bf16[1,64,18944]{2,1,0:T(8,128)(2,1)} reshape(bf16[64,32,592]{2,1,0:T(8,128)(2,1)S(1)} %copy.13) | data formatting | bytes 4849664 | tf_op jit(solution)/shard_map/reshape | solution.py:66
  379.0 1.0 slice_convert_fusion
  380.0 2.2 fusion.22
  383.1 1.0 fusion.31
  384.4 1.9 reshape.442
  386.8 27.5 %all_to_all.22 = bf16[32,64,320]{2,1,0:T(8,128)(2,1)S(1)} all-to-all(bf16[32,64,320]{2,1,0:T(8,128)(2,1)S(1)} %bitcast.96), channel_id=1, replica_groups=mesh['dp'=1,'fsdp'=32] {'fsdp'}, dimensions={0} | all-to-all | bytes 2621440 | tf_op jit(solution)/shard_map/all_to_all | solution.py:69
  414.4 8.1 %fusion.24 = f32[2048,2048]{1,0:T(8,128)} fusion(bf16[2048,320]{1,0:T(8,128)(2,1)S(1)} %bitcast.94, bf16[2,320,2048]{2,1,0:T(8,128)(2,1)S(1)} %copy-done.2), kind=kOutput, calls=%fused_computation.28 | convolution fusion | flops 2684354560 | bytes 19660800 | tf_op jit(solution)/shard_map/dot_general | solution.py:70
  423.2 104.9 %reduce-scatter.5.cloned.1.call-done = f32[64,2048]{1,0:T(8,128)} async-done(((f32[2048,2048]{1,0:T(8,128)}), f32[64,2048]{1,0:T(8,128)}) %reduce-scatter.5.cloned.1.call-update) | async-done | bytes 524304 | tf_op jit(solution)/shard_map/reduce_scatter | solution.py:71
  528.1 1.8 fusion.43
  (43 shorter events, 6.7 us)
Async XLA Ops:
  7.2 55.0 %all-gather.5.cloned.1.call-start = ((), (), s32[]{:S(2)}) async-start(), calls=%async_computation.8 | async-start | bytes 8650752 | tf_op jit(solution)/shard_map/all_gather | solution.py:63
  74.0 39.7 %all-to-all-start = ((bf16[32,64,592]{2,1,0:T(8,128)(2,1)}), bf16[32,64,592]{2,1,0:T(8,128)(2,1)S(1)}, u32[]{:S(2)}, u32[]{:S(2)}) async-start(bf16[32,64,592]{2,1,0:T(8,128)(2,1)} %bitcast.90), calls=%async_computation | async-start | bytes 5242880 | tf_op jit(solution)/shard_map/all_to_all | solution.py:65
  78.9 191.1 %reduce-scatter.3.cloned.1.call-start = ((), (), s32[]{:S(2)}) async-start(), calls=%async_computation.6 | async-start | bytes 17301504 | tf_op jit(solution)/shard_map/reduce_scatter | solution.py:71
  128.5 28.2 %copy-start.1 = (bf16[2,320,2048]{2,1,0:T(8,128)(2,1)S(1)}, bf16[2,320,2048]{2,1,0:T(8,128)(2,1)}, u32[]{:S(2)}) copy-start(bf16[2,320,2048]{2,1,0:T(8,128)(2,1)} %param.7) | copy-start | bytes 7864324
  164.7 105.3 %copy-start = (bf16[1,64,2048]{2,1,0:T(8,128)(2,1)S(1)}, bf16[1,64,2048]{2,1,0:T(8,128)(2,1)}, u32[]{:S(2)}) copy-start(bf16[1,64,2048]{2,1,0:T(8,128)(2,1)} %param.4) | copy-start | bytes 786436
  164.8 154.5 %all-gather.7.cloned.1.call-start = ((), (), s32[]{:S(2)}) async-start(), calls=%async_computation.9 | async-start | bytes 8650752 | tf_op jit(solution)/shard_map/all_gather | solution.py:63
  272.4 255.7 %reduce-scatter.5.cloned.1.call-start = ((), (), s32[]{:S(2)}) async-start(), calls=%async_computation.7 | async-start | bytes 17301504 | tf_op jit(solution)/shard_map/reduce_scatter | solution.py:71
  386.3 28.1 %copy-start.2 = (bf16[2,320,2048]{2,1,0:T(8,128)(2,1)S(1)}, bf16[2,320,2048]{2,1,0:T(8,128)(2,1)}, u32[]{:S(2)}) copy-start(bf16[2,320,2048]{2,1,0:T(8,128)(2,1)} %param.7) | copy-start | bytes 7864324
Sparse Core Ops, SparseCore 0:
  12.3 49.8 all-gather.4
  164.9 105.0 reduce-scatter.2
  272.7 46.6 all-gather.6
  422.6 105.3 reduce-scatter.4

commit v2 on v0

v2 whole, which is shorter than its diff:
```python
import functools
import math

import jax
import jax.numpy as jnp
from jax import lax
from jax.experimental import pallas as pl
from jax.experimental.pallas import tpu as pltpu
from jax.sharding import PartitionSpec as P

HEAD_DIM = 256
ROPE_BASE = 10000.0
NORM_EPS = 1e-6
LANES = 128
CORES = 2
MESH = pl.DeviceIdType.MESH


def rope_tables(seq_len):
    half_dim = HEAD_DIM // 2
    inv_freq = ROPE_BASE ** (-jnp.arange(half_dim, dtype=jnp.float32) / half_dim)
    angle = jnp.arange(seq_len, dtype=jnp.float32)[:, None] * inv_freq[None, :]
    return jnp.cos(angle), jnp.sin(angle)


GATHER, SEND_P, SEND_M, REDUCE, WEIGHT = 0, 40, 56, 72, 96
EVENTS = 98


def layer_kernel(ring, num_heads, x_ref, gain_ref, w_in_ref, w_out_ref, cos_ref, sin_ref, y_ref, k_ref, v_ref,
                 h_all, w_in_own, w_in_peer, w_out_all, p_out, p_in, mixed_out, mixed_in, part_y, part_x,
                 opp_lo, opp_hi, ring_lo, ring_hi, last_opp_lo, last_opp_hi, last_lo, last_hi,
                 send_sem, recv_sem, local_sem):
    tokens, d_model = x_ref.shape
    half, quarter = tokens // 2, tokens // 4
    d_half = d_model // 2
    out_part = w_out_ref.shape[0]
    chip_rows = CORES * out_part
    chip_cols = w_in_ref.shape[1]
    me = lax.axis_index("fsdp")
    core = lax.rem(me, CORES)
    chip = me // CORES
    x = lax.rem(chip, ring)
    y = chip // ring

    def wrap(a):
        return lax.rem(a + ring, ring)

    def device(cx, cy):
        return (wrap(cy) * ring + wrap(cx)) * CORES + core

    sends = []
    done = set()

    def send(event, src, dst, target):
        copy = pltpu.make_async_remote_copy(src_ref=src, dst_ref=dst, send_sem=send_sem.at[event],
                                            recv_sem=recv_sem.at[event], device_id={"fsdp": target},
                                            device_id_type=MESH)
        copy.start()
        sends.append(copy)

    def need(event, dst):
        if event in done:
            return
        done.add(event)
        pltpu.make_async_remote_copy(src_ref=dst, dst_ref=dst, send_sem=send_sem.at[event],
                                     recv_sem=recv_sem.at[event], device_id={"fsdp": me},
                                     device_id_type=MESH).wait_recv()

    peer = chip * CORES + (1 - core)
    barrier = pltpu.get_barrier_semaphore()
    pl.semaphore_signal(barrier, inc=1, device_id={"fsdp": peer}, device_id_type=MESH)
    others = [(dx, dy) for dy in range(ring) for dx in range(ring) if dx or dy]
    for dx, dy in others:
        pl.semaphore_signal(barrier, inc=1, device_id={"fsdp": device(x + dx, y + dy)}, device_id_type=MESH)

    local = [
        pltpu.make_async_copy(w_in_ref, w_in_own, local_sem.at[0]),
        pltpu.make_async_copy(w_out_ref, w_out_all.at[pl.ds(core * out_part, out_part)], local_sem.at[1]),
    ]
    for copy in local:
        copy.start()

    x_float = x_ref[...].astype(jnp.float32)
    centred = x_float - jnp.mean(x_float, axis=-1, keepdims=True)
    variance = jnp.mean(centred * centred, axis=-1, keepdims=True)
    normed = centred * lax.rsqrt(variance + NORM_EPS) * gain_ref[...].astype(jnp.float32)
    h_all[y, x] = normed.astype(jnp.bfloat16)

    pl.semaphore_wait(barrier, len(others) + 1)

    def place(part, prim, sec):
        return (x + prim, y + sec) if part == 0 else (x + sec, y + prim)

    def block(part, prim, sec, low, count):
        cx, cy = place(part, prim, sec)
        return h_all.at[wrap(cy), wrap(cx), pl.ds(part * half + low, count)]

    def gather_send(event, part, blk, prim, sec):
        send(event, blk, blk, device(*place(part, prim, sec)))

    steps = (0, -1, 1, 2)

    def base(part):
        return GATHER + 20 * part

    def to_second(part, j):
        e = base(part) + 4 + 4 * j
        blk = block(part, steps[j], 0, 0, half)
        gather_send(e, part, blk, 0, 1)
        gather_send(e + 1, part, blk, 0, -1)

    def got_first(part, which):
        e = base(part)
        if which == -1:
            need(e, block(part, -1, 0, 0, half))
        elif which == 1:
            need(e + 1, block(part, 1, 0, 0, half))
        else:
            need(e + 2, block(part, 2, 0, 0, quarter))
            need(e + 3, block(part, 2, 0, quarter, quarter))

    def got_second(part, j, which):
        e = base(part) + 4 + 4 * j
        dp = steps[j]
        if which == -1:
            need(e, block(part, dp, -1, 0, half))
        elif which == 1:
            need(e + 1, block(part, dp, 1, 0, half))
        else:
            need(e + 2, block(part, dp, 2, 0, quarter))
            need(e + 3, block(part, dp, 2, quarter, quarter))

    def pass_second(part, j):
        e = base(part) + 4 + 4 * j
        dp = steps[j]
        got_second(part, j, -1)
        gather_send(e + 2, part, block(part, dp, -1, 0, quarter), 0, 1)
        got_second(part, j, 1)
        gather_send(e + 3, part, block(part, dp, 1, quarter, quarter), 0, -1)

    for part in (0, 1):
        own = block(part, 0, 0, 0, half)
        gather_send(base(part), part, own, 1, 0)
        gather_send(base(part) + 1, part, own, -1, 0)
    for part in (0, 1):
        to_second(part, 0)
    send(WEIGHT, w_in_ref, w_in_peer, peer)
    send(WEIGHT + 1, w_out_ref, w_out_all.at[pl.ds(core * out_part, out_part)], peer)
    for part in (0, 1):
        got_first(part, -1)
        gather_send(base(part) + 2, part, block(part, -1, 0, 0, quarter), 1, 0)
        got_first(part, 1)
        gather_send(base(part) + 3, part, block(part, 1, 0, quarter, quarter), -1, 0)
    for part in (0, 1):
        to_second(part, 1)
        to_second(part, 2)
    for part in (0, 1):
        pass_second(part, 0)
    for part in (0, 1):
        got_first(part, 2)
        to_second(part, 3)

    local[0].wait()
    need(WEIGHT, w_in_peer)
    strip = min(d_model, 256)

    @pl.loop(0, d_model // strip)
    def _(i):
        rows = pl.ds(pl.multiple_of(i * strip, strip), strip)
        w_in_own[rows] = w_in_own[rows] + w_in_peer[rows]

    wide = math.gcd(chip_cols, 256)

    def row_product(dy):
        row = wrap(y + dy)
        lhs = h_all[row].reshape(ring * tokens, d_model)

        @pl.loop(0, chip_cols // wide)
        def _(n):
            cols = pl.ds(pl.multiple_of(n * wide, wide), wide)
            res = jnp.dot(lhs, w_in_own[:, cols], preferred_element_type=jnp.float32)
            p_out[row, :, :, cols] = res.astype(jnp.bfloat16).reshape(ring, tokens, wide)

        for dx in (2, 1, 3, 0):
            col = wrap(x + dx)
            if dx == 0 and dy == 0:
                p_in[y, x] = p_out[y, x]
            else:
                send(SEND_P + (dy % ring) * ring + dx, p_out.at[row, col], p_in.at[y, x], device(x + dx, y + dy))

    for which in (-1, 1, 2):
        got_second(1, 0, which)
    row_product(0)
    for j in (1, 2):
        for part in (0, 1):
            pass_second(part, j)
    for part in (0, 1):
        pass_second(part, 3)
    for dy, j in ((-1, 1), (1, 2), (2, 3)):
        for i in range(ring):
            got_second(0, i, dy)
        for which in (-1, 1, 2):
            got_second(1, j, which)
        row_product(dy)

    for dx, dy in others:
        need(SEND_P + dy * ring + dx, p_in.at[wrap(y - dy), wrap(x - dx)])

    real_cols = chip_cols_real(w_in_ref, ring, num_heads, out_part)

    def tile(t):
        pieces = []
        for c in range(ring * ring):
            if c * real_cols < (t + 1) * LANES and (c + 1) * real_cols > t * LANES:
                low = (t - (c * real_cols) // LANES) * LANES
                pieces.append(p_in[c // ring, c % ring, :, low:low + LANES])
        return sum(pieces[1:], pieces[0])

    cos_table = cos_ref[...]
    sin_table = sin_ref[...]

    def rotated(t, scale):
        first = tile(t).astype(jnp.float32)
        second = tile(t + 1).astype(jnp.float32)
        a = first * cos_table - second * sin_table
        b = second * cos_table + first * sin_table
        return jnp.concatenate([(a * scale).astype(jnp.bfloat16), (b * scale).astype(jnp.bfloat16)], axis=-1)

    head_tiles = HEAD_DIM // LANES
    q_tiles = num_heads * head_tiles
    out_tiles = chip_rows // LANES

    def put(t, val):
        c, i = divmod(t, out_tiles)
        mixed_out[c, :, i * LANES:(i + 1) * LANES] = val

    query = jnp.concatenate([rotated(h * head_tiles, HEAD_DIM ** -0.5) for h in range(num_heads)], axis=0)
    key = rotated(q_tiles, 1.0)
    value = jnp.concatenate([tile(q_tiles + 2), tile(q_tiles + 3)], axis=-1)
    k_ref[...] = key
    v_ref[...] = value
    scores = lax.dot_general(query, key, (((1,), (1,)), ((), ())), preferred_element_type=jnp.float32)
    scores = scores.reshape(num_heads, tokens, tokens)
    q_pos = lax.broadcasted_iota(jnp.int32, scores.shape, 1)
    k_pos = lax.broadcasted_iota(jnp.int32, scores.shape, 2)
    scores = jnp.where(q_pos >= k_pos, scores, -1e30)
    weight = jnp.exp(scores - jnp.max(scores, axis=-1, keepdims=True))
    row_sum = jnp.sum(weight, axis=-1, keepdims=True)
    attended = jnp.dot(weight.astype(jnp.bfloat16).reshape(num_heads * tokens, tokens), value,
                       preferred_element_type=jnp.float32).reshape(num_heads, tokens, HEAD_DIM)
    attended = (attended / row_sum).astype(jnp.bfloat16)
    for h in range(num_heads):
        for i in range(head_tiles):
            put(h * head_tiles + i, attended[h, :, i * LANES:(i + 1) * LANES])
    ff_tiles = ring * ring * out_tiles - q_tiles
    for t in range(ff_tiles):
        gate = tile(q_tiles + 4 + t).astype(jnp.float32)
        up = tile(q_tiles + 4 + ff_tiles + t).astype(jnp.float32)
        put(q_tiles + t, (jax.nn.silu(gate) * up).astype(jnp.bfloat16))

    far_first = sorted(others, key=lambda d: -((d[0] == 2) + (d[1] == 2)))
    for dx, dy in far_first:
        send(SEND_M + dy * ring + dx, mixed_out.at[wrap(y + dy) * ring + wrap(x + dx)], mixed_in.at[y, x],
             device(x + dx, y + dy))
    mixed_in[y, x] = mixed_out[chip]
    local[1].wait()
    need(WEIGHT + 1, w_out_all.at[pl.ds((1 - core) * out_part, out_part)])

    parts = (part_y, part_x)
    centre = ((y, x), (x, y))

    def lined(f, prim, sec):
        return (x + sec, y + prim) if f == 0 else (x + prim, y + sec)

    def arrived(f, prim):
        for sec in range(ring):
            dx, dy = (-sec, -prim) if f == 0 else (-prim, -sec)
            dx, dy = dx % ring, dy % ring
            if dx or dy:
                need(SEND_M + dy * ring + dx, mixed_in.at[wrap(y - dy), wrap(x - dx)])

    narrow = min(d_half, 256)

    def product(f, prim):
        arrived(f, prim)
        idx = wrap(centre[f][0] + prim)
        lhs = mixed_in[idx] if f == 0 else mixed_in[:, idx]
        lhs = lhs.reshape(ring * tokens, chip_rows)

        @pl.loop(0, d_half // narrow)
        def _(n):
            src = pl.ds(pl.multiple_of(f * d_half + n * narrow, narrow), narrow)
            cols = pl.ds(pl.multiple_of(n * narrow, narrow), narrow)
            res = jnp.dot(lhs, w_out_all[:, src], preferred_element_type=jnp.float32)
            parts[f][idx, :, :, cols] = res.reshape(ring, tokens, narrow)

    lo, hi = pl.ds(0, ring // 2), pl.ds(ring // 2, ring // 2)
    t_lo, t_hi = pl.ds(0, half), pl.ds(half, half)

    def event(f, i):
        return REDUCE + 12 * f + i

    def at(f, prim):
        return wrap(centre[f][0] + prim)

    def toward(f, prim, sec):
        return device(*lined(f, prim, sec))

    for f in (0, 1):
        product(f, 2)
        send(event(f, 0), parts[f].at[at(f, 2), lo], opp_lo.at[f], toward(f, 1, 0))
        send(event(f, 1), parts[f].at[at(f, 2), hi], opp_hi.at[f], toward(f, -1, 0))
    for f in (0, 1):
        product(f, 1)
        send(event(f, 2), parts[f].at[at(f, 1), hi], ring_lo.at[f, hi], toward(f, 1, 0))
        product(f, -1)
        send(event(f, 3), parts[f].at[at(f, -1), lo], ring_hi.at[f, lo], toward(f, -1, 0))
    for f in (0, 1):
        product(f, 0)
    for f in (0, 1):
        need(event(f, 0), opp_lo.at[f])
        parts[f][at(f, 1), lo] = parts[f][at(f, 1), lo] + opp_lo[f]
        send(event(f, 4), parts[f].at[at(f, 1), lo], ring_lo.at[f, lo], toward(f, 1, 0))
        need(event(f, 1), opp_hi.at[f])
        parts[f][at(f, -1), hi] = parts[f][at(f, -1), hi] + opp_hi[f]
        send(event(f, 5), parts[f].at[at(f, -1), hi], ring_hi.at[f, hi], toward(f, -1, 0))

    def second(f, sec):
        return wrap(centre[f][1] + sec)

    for f in (0, 1):
        need(event(f, 2), ring_lo.at[f, hi])
        need(event(f, 3), ring_hi.at[f, lo])
        need(event(f, 4), ring_lo.at[f, lo])
        need(event(f, 5), ring_hi.at[f, hi])
        mid = at(f, 0)
        parts[f][mid] = parts[f][mid] + ring_lo[f] + ring_hi[f]
        send(event(f, 6), parts[f].at[mid, second(f, 2), t_lo], last_opp_lo.at[f], toward(f, 0, 1))
        send(event(f, 7), parts[f].at[mid, second(f, 2), t_hi], last_opp_hi.at[f], toward(f, 0, -1))
        send(event(f, 8), parts[f].at[mid, second(f, 1), t_hi], last_lo.at[f, t_hi], toward(f, 0, 1))
        send(event(f, 9), parts[f].at[mid, second(f, -1), t_lo], last_hi.at[f, t_lo], toward(f, 0, -1))
    for f in (0, 1):
        mid = at(f, 0)
        need(event(f, 6), last_opp_lo.at[f])
        parts[f][mid, second(f, 1), t_lo] = parts[f][mid, second(f, 1), t_lo] + last_opp_lo[f]
        send(event(f, 10), parts[f].at[mid, second(f, 1), t_lo], last_lo.at[f, t_lo], toward(f, 0, 1))
        need(event(f, 7), last_opp_hi.at[f])
        parts[f][mid, second(f, -1), t_hi] = parts[f][mid, second(f, -1), t_hi] + last_opp_hi[f]
        send(event(f, 11), parts[f].at[mid, second(f, -1), t_hi], last_hi.at[f, t_hi], toward(f, 0, -1))
    for f in (0, 1):
        need(event(f, 8), last_lo.at[f, t_hi])
        need(event(f, 9), last_hi.at[f, t_lo])
        need(event(f, 10), last_lo.at[f, t_lo])
        need(event(f, 11), last_hi.at[f, t_hi])
        out_sum = parts[f][at(f, 0), second(f, 0)] + last_lo[f] + last_hi[f]
        cols = slice(f * d_half, (f + 1) * d_half)
        y_ref[:, cols] = (x_ref[:, cols].astype(jnp.float32) + out_sum).astype(jnp.bfloat16)
    for copy in sends:
        copy.wait_send()


def chip_cols_real(w_in_ref, ring, num_heads, out_part):
    ff_dim = ring * ring * CORES * out_part - num_heads * HEAD_DIM
    return (num_heads * HEAD_DIM + 2 * HEAD_DIM + 2 * ff_dim) // (ring * ring)


def parallel_layer(hidden, gain_vec, w_in_place, w_out_part, tables, ring, num_heads):
    batch, tokens, d_model = hidden.shape
    padded_cols = w_in_place.shape[1]
    out_part = w_out_part.shape[0]
    chip_rows = CORES * out_part
    d_half = d_model // 2
    bf16, f32 = jnp.bfloat16, jnp.float32
    vmem = pl.BlockSpec(memory_space=pltpu.VMEM)
    anywhere = pl.BlockSpec(memory_space=pl.ANY)
    out, k_rot, value = pl.pallas_call(
        functools.partial(layer_kernel, ring, num_heads),
        out_shape=(
            jax.ShapeDtypeStruct((tokens, d_model), bf16),
            jax.ShapeDtypeStruct((tokens, HEAD_DIM), bf16),
            jax.ShapeDtypeStruct((tokens, HEAD_DIM), bf16),
        ),
        in_specs=[vmem, vmem, anywhere, anywhere, vmem, vmem],
        out_specs=(vmem, vmem, vmem),
        scratch_shapes=[
            pltpu.VMEM((ring, ring, tokens, d_model), bf16),
            pltpu.VMEM((d_model, padded_cols), bf16),
            pltpu.VMEM((d_model, padded_cols), bf16),
            pltpu.VMEM((chip_rows, d_model), bf16),
            pltpu.VMEM((ring, ring, tokens, padded_cols), bf16),
            pltpu.VMEM((ring, ring, tokens, padded_cols), bf16),
            pltpu.VMEM((ring * ring, tokens, chip_rows), bf16),
            pltpu.VMEM((ring, ring, tokens, chip_rows), bf16),
            pltpu.VMEM((ring, ring, tokens, d_half), f32),
            pltpu.VMEM((ring, ring, tokens, d_half), f32),
            pltpu.VMEM((2, ring // 2, tokens, d_half), f32),
            pltpu.VMEM((2, ring // 2, tokens, d_half), f32),
            pltpu.VMEM((2, ring, tokens, d_half), f32),
            pltpu.VMEM((2, ring, tokens, d_half), f32),
            pltpu.VMEM((2, tokens // 2, d_half), f32),
            pltpu.VMEM((2, tokens // 2, d_half), f32),
            pltpu.VMEM((2, tokens, d_half), f32),
            pltpu.VMEM((2, tokens, d_half), f32),
            pltpu.SemaphoreType.DMA((EVENTS,)),
            pltpu.SemaphoreType.DMA((EVENTS,)),
            pltpu.SemaphoreType.DMA((2,)),
        ],
        compiler_params=pltpu.CompilerParams(collective_id=0, has_side_effects=True, vmem_limit_bytes=62 * 2 ** 20),
        name="layer",
    )(hidden.reshape(tokens, d_model), gain_vec.reshape(1, d_model), w_in_place, w_out_part, *tables)
    return out.reshape(hidden.shape), k_rot.reshape(batch, tokens, HEAD_DIM), value.reshape(batch, tokens, HEAD_DIM)


def solution(mesh):
    batch_axes = ("dp", "fsdp")
    group = mesh.shape["fsdp"]
    ring = math.isqrt(group // CORES)
    if ring != 4 or ring * ring * CORES != group:
        raise ValueError("unsupported group")

    def device_program(x_local, gain, w_in_local, w_out_local):
        layers, d_model, in_part = w_in_local.shape
        out_rows = w_out_local.shape[1] * group
        ff_dim = in_part * group - out_rows - 2 * HEAD_DIM
        num_heads = (out_rows - ff_dim) // HEAD_DIM
        chip_cols = CORES * in_part
        phases = max((chip_cols * c) % LANES for c in range(ring * ring))
        padded = -(-(chip_cols + phases) // LANES) * LANES
        me = lax.axis_index("fsdp")
        offset = lax.rem(chip_cols * (me // CORES), LANES) + in_part * lax.rem(me, CORES)
        hidden = x_local
        tables = rope_tables(x_local.shape[1])
        key_list = []
        value_list = []
        for layer in range(layers):
            w_in_place = lax.dynamic_update_slice(jnp.zeros((d_model, padded), w_in_local.dtype), w_in_local[layer],
                                                  (0, offset))
            hidden, k_rot, value = parallel_layer(hidden, gain[layer], w_in_place, w_out_local[layer], tables, ring,
                                                  num_heads)
            key_list.append(k_rot)
            value_list.append(value)
        return hidden, jnp.stack(key_list), jnp.stack(value_list)

    return jax.shard_map(
        device_program,
        mesh=mesh,
        in_specs=(P(batch_axes, None, None), P(None, None), P(None, None, "fsdp"), P(None, "fsdp", None)),
        out_specs=(P(batch_axes, None, None), P(None, batch_axes, None, None), P(None, batch_axes, None, None)),
        check_vma=False,
    )
```

time: 754 us -> 340 us (0.45)
  waiting for transfers between devices: 625 us -> 0 us
  Pallas kernels: 0 us -> 266 us
  matrix products: 102 us -> 0 us
  local copies, waits for them, and re-layouts: 7.9 us -> 69.7 us
  between operations: 14 us -> 0.71 us
    all_gather x4 -> x0, waiting for transfers between devices: 623 us -> none  [the longest x2 427 us: device_program(): w_in_full = lax.all_gather(w_in_local[layer], 'fsdp', axis=1, tiled=True)]
    pallas_call x0 -> x2, Pallas kernels: none -> 266 us  [parallel_layer(): pl.pallas_call(functools.partial(layer_kernel, ring, num_heads), out_shap...]
    dot_general x10 -> x0, matrix products: 102 us -> none  [the longest x2 62.4 us: parallel_layer(): jnp.einsum('bsd,de->bse', normed, w_in_full, preferred_element_type=jnp.f...]
    dynamic_update_slice x0 -> x2, local copies, waits for them, and re-layouts: none -> 47 us  [device_program(): lax.dynamic_update_slice(jnp.zeros((d_model, padded), w_in_local.dtype),...]
  transfers between devices with their start and end apart: 4 -> 0, of which waited for: 4 -> 0; matrix products, arithmetic and copies ran while one was open for 12% -> 0% of each run, Pallas kernels for 0% -> 0%
where the time goes in v2:
time: 340 us; the launch traced here: 338 us
  Pallas kernels  266 us (78%)
  local copies, waits for them, and re-layouts  69.7 us (20%)
    pallas_call x2, Pallas kernels, parallel_layer(): pl.pallas_call(functools.partial(layer_kernel, ring, num_heads), out_shap...  266 us
    dynamic_update_slice x2, local copies, waits for them, and re-layouts, device_program(): lax.dynamic_update_slice(jnp.zeros((d_model, padded), w_in_local.dtype),...  47 us
    unnamed x9, local copies, waits for them, and re-layouts  7.87 us

profile of v2, /device:TPU:96, one launch (start us, length us, event | category | flops | bytes accessed | tf_op | source)
XLA Modules:
  0.0 338.2 jit_solution(5063000666150577473)
XLA Ops:
  0.7 5.3 %fusion.2 = (bf16[1,2048,592]{1,2,0:T(8,128)(2,1)}, bf16[1,2048,592]{1,2,0:T(8,128)(2,1)}) fusion(bf16[2,2048,592]{1,2,0:T(8,128)(2,1)} %param.6), kind=kLoop, calls=%fused_computation.8 | loop fusion | bytes 9699328 | tf_op jit(solution)/shard_map/slice | solution.py:437
  6.0 3.1 copy.9
  9.1 2.6 broadcast.14.clone
  11.7 23.5 %dynamic_update_slice.6.w_in_ref = bf16[2048,1280]{1,0:T(8,128)(2,1)} dynamic-update-slice(bf16[2048,1280]{1,0:T(8,128)(2,1)} %broadcast.14.clone, bf16[2048,592]{1,0:T(8,128)(2,1)S(1)} %bitcast.13, s32[]{:T(128)} %constant.26.clone.1, s32[]{:T(128)S(6)} %select_n.10) | dynamic-update-slice | bytes 4849668 | tf_op jit(solution)/shard_map/dynamic_update_slice | solution.py:437
  35.2 0.8 fusion
  36.0 0.0 copy-start
  36.0 3.6 %slice_bitcast_fusion = (bf16[320,2048]{1,0:T(8,128)(2,1)}, bf16[320,2048]{1,0:T(8,128)(2,1)}) fusion(bf16[2,320,2048]{2,1,0:T(8,128)(2,1)} %param.7), kind=kLoop, calls=%fused_computation | loop fusion | bytes 5242880 | tf_op jit(solution)/shard_map/squeeze | solution.py:439
  39.6 0.0 copy-done
  39.6 0.6 fusion.3
  40.2 134.2 %layer.2 = (bf16[64,2048]{1,0:T(8,128)(2,1)}, bf16[64,256]{1,0:T(8,128)(2,1)}, bf16[64,256]{1,0:T(8,128)(2,1)}) custom-call(bf16[64,2048]{1,0:T(8,128)(2,1)} %bitcast.15, bf16[1,2048]{1,0:T(2,128)(2,1)} %get-tuple-element.20.gain_ref, bf16[2048,1280]{1,0:T(8,128)(2,1)} %dynamic_update_slice.6.w_in_ref, bf16[320,2048]{1,0:T(8,128)(2,1)} %get-tuple-element.18.w_out_ref, ...), custom_call_target="tpu_custom_call" | custom-call | tf_op jit(solution)/shard_map/layer/pallas_call | solution.py:377
  174.4 3.1 copy.10
  177.5 2.6 broadcast.14.clone.1
  180.2 23.5 %dynamic_update_slice.7.w_in_ref = bf16[2048,1280]{1,0:T(8,128)(2,1)} dynamic-update-slice(bf16[2048,1280]{1,0:T(8,128)(2,1)} %broadcast.14.clone.1, bf16[2048,592]{1,0:T(8,128)(2,1)S(1)} %bitcast.12, s32[]{:T(128)} %constant.26.clone.1, s32[]{:T(128)S(6)} %select_n.10) | dynamic-update-slice | bytes 4849668 | tf_op jit(solution)/shard_map/dynamic_update_slice | solution.py:437
  203.7 0.0 copy-start.1
  203.7 0.0 copy-start.2
  203.7 131.4 %layer.3 = (bf16[64,2048]{1,0:T(8,128)(2,1)}, bf16[64,256]{1,0:T(8,128)(2,1)}, bf16[64,256]{1,0:T(8,128)(2,1)}) custom-call(bf16[64,2048]{1,0:T(8,128)(2,1)} %get-tuple-element.9.x_ref, bf16[1,2048]{1,0:T(2,128)(2,1)} %get-tuple-element.19.gain_ref, bf16[2048,1280]{1,0:T(8,128)(2,1)} %dynamic_update_slice.7.w_in_ref, ...), custom_call_target="tpu_custom_call" | custom-call | tf_op jit(solution)/shard_map/layer/pallas_call | solution.py:377
  335.1 0.0 copy-done.1
  335.1 0.0 copy-done.2
  335.1 1.4 pad_maximum_fusion
  336.6 1.7 copy.14
  (1 shorter events, 0.0 us)
Async XLA Ops:
  36.0 3.6 %copy-start = (bf16[2,2048]{1,0:T(2,128)(2,1)S(1)}, bf16[2,2048]{1,0:T(2,128)(2,1)}, u32[]{:S(2)}) copy-start(bf16[2,2048]{1,0:T(2,128)(2,1)} %param.5) | copy-start | bytes 24580
  203.7 131.4 %copy-start.1 = (bf16[64,256]{1,0:T(8,128)(2,1)S(1)}, bf16[64,256]{1,0:T(8,128)(2,1)}, u32[]{:S(2)}) copy-start(bf16[64,256]{1,0:T(8,128)(2,1)} %get-tuple-element.11) | copy-start | bytes 98308
  203.7 131.5 %copy-start.2 = (bf16[64,256]{1,0:T(8,128)(2,1)S(1)}, bf16[64,256]{1,0:T(8,128)(2,1)}, u32[]{:S(2)}) copy-start(bf16[64,256]{1,0:T(8,128)(2,1)} %get-tuple-element.13) | copy-start | bytes 98308

commit v3 on v2

--- a/solution.py
+++ b/solution.py
@@ -6,6 +6,7 @@
 from jax import lax
 from jax.experimental import pallas as pl
 from jax.experimental.pallas import tpu as pltpu
+import numpy as np
 from jax.sharding import PartitionSpec as P
 
 HEAD_DIM = 256
@@ -18,25 +19,27 @@
 
 def rope_tables(seq_len):
     half_dim = HEAD_DIM // 2
-    inv_freq = ROPE_BASE ** (-jnp.arange(half_dim, dtype=jnp.float32) / half_dim)
-    angle = jnp.arange(seq_len, dtype=jnp.float32)[:, None] * inv_freq[None, :]
-    return jnp.cos(angle), jnp.sin(angle)
+    inv_freq = np.float32(ROPE_BASE) ** (-np.arange(half_dim, dtype=np.float32) / np.float32(half_dim))
+    angle = np.arange(seq_len, dtype=np.float32)[:, None] * inv_freq[None, :].astype(np.float32)
+    return jnp.asarray(np.cos(angle), jnp.float32), jnp.asarray(np.sin(angle), jnp.float32)
 
 
 GATHER, SEND_P, SEND_M, REDUCE, WEIGHT = 0, 40, 56, 72, 96
 EVENTS = 98
 
 
-def layer_kernel(ring, num_heads, x_ref, gain_ref, w_in_ref, w_out_ref, cos_ref, sin_ref, y_ref, k_ref, v_ref,
-                 h_all, w_in_own, w_in_peer, w_out_all, p_out, p_in, mixed_out, mixed_in, part_y, part_x,
+def layer_kernel(ring, num_heads, layer, x_ref, gain_ref, w_in_ref, w_out_ref, cos_ref, sin_ref, y_ref, k_ref, v_ref,
+                 h_all, w_in_all, w_out_all, p_out, p_in, mixed_out, mixed_in, part_y, part_x,
                  opp_lo, opp_hi, ring_lo, ring_hi, last_opp_lo, last_opp_hi, last_lo, last_hi,
                  send_sem, recv_sem, local_sem):
     tokens, d_model = x_ref.shape
     half, quarter = tokens // 2, tokens // 4
     d_half = d_model // 2
-    out_part = w_out_ref.shape[0]
+    in_part = w_in_ref.shape[1]
+    out_part = w_out_ref.shape[1]
     chip_rows = CORES * out_part
-    chip_cols = w_in_ref.shape[1]
+    real_cols = CORES * in_part
+    chip_cols = w_in_all.shape[0]
     me = lax.axis_index("fsdp")
     core = lax.rem(me, CORES)
     chip = me // CORES
@@ -67,6 +70,11 @@
                                      recv_sem=recv_sem.at[event], device_id={"fsdp": me},
                                      device_id_type=MESH).wait_recv()
 
+    margin = chip_cols - real_cols
+    if margin:
+        w_in_all[0:margin] = jnp.zeros((margin, d_model), w_in_all.dtype)
+        w_in_all[real_cols:chip_cols] = jnp.zeros((margin, d_model), w_in_all.dtype)
+
     peer = chip * CORES + (1 - core)
     barrier = pltpu.get_barrier_semaphore()
     pl.semaphore_signal(barrier, inc=1, device_id={"fsdp": peer}, device_id_type=MESH)
@@ -74,9 +82,17 @@
     for dx, dy in others:
         pl.semaphore_signal(barrier, inc=1, device_id={"fsdp": device(x + dx, y + dy)}, device_id_type=MESH)
 
+    phase = lax.rem(real_cols * chip, LANES)
+
+    def in_rows(which):
+        return w_in_all.at[pl.ds(pl.multiple_of(phase + which * in_part, 16), in_part)]
+
+    def out_rows(which):
+        return w_out_all.at[pl.ds(pl.multiple_of(which * out_part, 16), out_part)]
+
     local = [
-        pltpu.make_async_copy(w_in_ref, w_in_own, local_sem.at[0]),
-        pltpu.make_async_copy(w_out_ref, w_out_all.at[pl.ds(core * out_part, out_part)], local_sem.at[1]),
+        pltpu.make_async_copy(w_in_ref.at[layer], in_rows(core), local_sem.at[0]),
+        pltpu.make_async_copy(w_out_ref.at[layer], out_rows(core), local_sem.at[1]),
     ]
     for copy in local:
         copy.start()
@@ -84,7 +100,7 @@
     x_float = x_ref[...].astype(jnp.float32)
     centred = x_float - jnp.mean(x_float, axis=-1, keepdims=True)
     variance = jnp.mean(centred * centred, axis=-1, keepdims=True)
-    normed = centred * lax.rsqrt(variance + NORM_EPS) * gain_ref[...].astype(jnp.float32)
+    normed = centred * lax.rsqrt(variance + NORM_EPS) * gain_ref[layer:layer + 1].astype(jnp.float32)
     h_all[y, x] = normed.astype(jnp.bfloat16)
 
     pl.semaphore_wait(barrier, len(others) + 1)
@@ -145,8 +161,8 @@
         gather_send(base(part) + 1, part, own, -1, 0)
     for part in (0, 1):
         to_second(part, 0)
-    send(WEIGHT, w_in_ref, w_in_peer, peer)
-    send(WEIGHT + 1, w_out_ref, w_out_all.at[pl.ds(core * out_part, out_part)], peer)
+    send(WEIGHT, w_in_ref.at[layer], in_rows(core), peer)
+    send(WEIGHT + 1, w_out_ref.at[layer], out_rows(core), peer)
     for part in (0, 1):
         got_first(part, -1)
         gather_send(base(part) + 2, part, block(part, -1, 0, 0, quarter), 1, 0)
@@ -162,13 +178,7 @@
         to_second(part, 3)
 
     local[0].wait()
-    need(WEIGHT, w_in_peer)
-    strip = min(d_model, 256)
-
-    @pl.loop(0, d_model // strip)
-    def _(i):
-        rows = pl.ds(pl.multiple_of(i * strip, strip), strip)
-        w_in_own[rows] = w_in_own[rows] + w_in_peer[rows]
+    need(WEIGHT, in_rows(1 - core))
 
     wide = math.gcd(chip_cols, 256)
 
@@ -179,9 +189,11 @@
         @pl.loop(0, chip_cols // wide)
         def _(n):
             cols = pl.ds(pl.multiple_of(n * wide, wide), wide)
-            res = jnp.dot(lhs, w_in_own[:, cols], preferred_element_type=jnp.float32)
+            res = lax.dot_general(lhs, w_in_all[cols], (((1,), (1,)), ((), ())), preferred_element_type=jnp.float32)
             p_out[row, :, :, cols] = res.astype(jnp.bfloat16).reshape(ring, tokens, wide)
 
+    def row_send(dy):
+        row = wrap(y + dy)
         for dx in (2, 1, 3, 0):
             col = wrap(x + dx)
             if dx == 0 and dy == 0:
@@ -197,17 +209,17 @@
             pass_second(part, j)
     for part in (0, 1):
         pass_second(part, 3)
+    row_send(0)
     for dy, j in ((-1, 1), (1, 2), (2, 3)):
         for i in range(ring):
             got_second(0, i, dy)
         for which in (-1, 1, 2):
             got_second(1, j, which)
         row_product(dy)
+        row_send(dy)
 
     for dx, dy in others:
         need(SEND_P + dy * ring + dx, p_in.at[wrap(y - dy), wrap(x - dx)])
-
-    real_cols = chip_cols_real(w_in_ref, ring, num_heads, out_part)
 
     def tile(t):
         pieces = []
@@ -235,6 +247,31 @@
         c, i = divmod(t, out_tiles)
         mixed_out[c, :, i * LANES:(i + 1) * LANES] = val
 
+    ff_tiles = ring * ring * out_tiles - q_tiles
+    for t in range(ff_tiles):
+        gate = tile(q_tiles + 4 + t).astype(jnp.float32)
+        up = tile(q_tiles + 4 + ff_tiles + t).astype(jnp.float32)
+        put(q_tiles + t, (jax.nn.silu(gate) * up).astype(jnp.bfloat16))
+
+    far_first = sorted(others, key=lambda d: -((d[0] == 2) + (d[1] == 2)))
+    first_plain = -(-q_tiles // out_tiles)
+
+    def mixed_send(plain):
+        for dx, dy in far_first:
+            dest = wrap(y + dy) * ring + wrap(x + dx)
+            copy = pltpu.make_async_remote_copy(
+                src_ref=mixed_out.at[dest], dst_ref=mixed_in.at[y, x], send_sem=send_sem.at[SEND_M + dy * ring + dx],
+                recv_sem=recv_sem.at[SEND_M + dy * ring + dx], device_id={"fsdp": device(x + dx, y + dy)},
+                device_id_type=MESH)
+
+            @pl.when(dest >= first_plain if plain else dest < first_plain)
+            def _():
+                copy.start()
+
+            if not plain:
+                sends.append(copy)
+
+    mixed_send(True)
     query = jnp.concatenate([rotated(h * head_tiles, HEAD_DIM ** -0.5) for h in range(num_heads)], axis=0)
     key = rotated(q_tiles, 1.0)
     value = jnp.concatenate([tile(q_tiles + 2), tile(q_tiles + 3)], axis=-1)
@@ -253,19 +290,10 @@
     for h in range(num_heads):
         for i in range(head_tiles):
             put(h * head_tiles + i, attended[h, :, i * LANES:(i + 1) * LANES])
-    ff_tiles = ring * ring * out_tiles - q_tiles
-    for t in range(ff_tiles):
-        gate = tile(q_tiles + 4 + t).astype(jnp.float32)
-        up = tile(q_tiles + 4 + ff_tiles + t).astype(jnp.float32)
-        put(q_tiles + t, (jax.nn.silu(gate) * up).astype(jnp.bfloat16))
-
-    far_first = sorted(others, key=lambda d: -((d[0] == 2) + (d[1] == 2)))
-    for dx, dy in far_first:
-        send(SEND_M + dy * ring + dx, mixed_out.at[wrap(y + dy) * ring + wrap(x + dx)], mixed_in.at[y, x],
-             device(x + dx, y + dy))
+    mixed_send(False)
     mixed_in[y, x] = mixed_out[chip]
     local[1].wait()
-    need(WEIGHT + 1, w_out_all.at[pl.ds((1 - core) * out_part, out_part)])
+    need(WEIGHT + 1, out_rows(1 - core))
 
     parts = (part_y, part_x)
     centre = ((y, x), (x, y))
@@ -360,22 +388,19 @@
         copy.wait_send()
 
 
-def chip_cols_real(w_in_ref, ring, num_heads, out_part):
-    ff_dim = ring * ring * CORES * out_part - num_heads * HEAD_DIM
-    return (num_heads * HEAD_DIM + 2 * HEAD_DIM + 2 * ff_dim) // (ring * ring)
-
-
-def parallel_layer(hidden, gain_vec, w_in_place, w_out_part, tables, ring, num_heads):
+def parallel_layer(hidden, gain, w_in_rows, w_out_part, tables, ring, num_heads, layer):
     batch, tokens, d_model = hidden.shape
-    padded_cols = w_in_place.shape[1]
-    out_part = w_out_part.shape[0]
+    out_part = w_out_part.shape[1]
+    real_cols = CORES * w_in_rows.shape[1]
+    margin = max((real_cols * c) % LANES for c in range(ring * ring))
+    padded_cols = -(-(real_cols + margin) // LANES) * LANES
     chip_rows = CORES * out_part
     d_half = d_model // 2
     bf16, f32 = jnp.bfloat16, jnp.float32
     vmem = pl.BlockSpec(memory_space=pltpu.VMEM)
     anywhere = pl.BlockSpec(memory_space=pl.ANY)
     out, k_rot, value = pl.pallas_call(
-        functools.partial(layer_kernel, ring, num_heads),
+        functools.partial(layer_kernel, ring, num_heads, layer),
         out_shape=(
             jax.ShapeDtypeStruct((tokens, d_model), bf16),
             jax.ShapeDtypeStruct((tokens, HEAD_DIM), bf16),
@@ -385,8 +410,7 @@
         out_specs=(vmem, vmem, vmem),
         scratch_shapes=[
             pltpu.VMEM((ring, ring, tokens, d_model), bf16),
-            pltpu.VMEM((d_model, padded_cols), bf16),
-            pltpu.VMEM((d_model, padded_cols), bf16),
+            pltpu.VMEM((padded_cols, d_model), bf16),
             pltpu.VMEM((chip_rows, d_model), bf16),
             pltpu.VMEM((ring, ring, tokens, padded_cols), bf16),
             pltpu.VMEM((ring, ring, tokens, padded_cols), bf16),
@@ -406,9 +430,9 @@
             pltpu.SemaphoreType.DMA((EVENTS,)),
             pltpu.SemaphoreType.DMA((2,)),
         ],
-        compiler_params=pltpu.CompilerParams(collective_id=0, has_side_effects=True, vmem_limit_bytes=62 * 2 ** 20),
+        compiler_params=pltpu.CompilerParams(collective_id=layer, has_side_effects=True, vmem_limit_bytes=62 * 2 ** 20),
         name="layer",
-    )(hidden.reshape(tokens, d_model), gain_vec.reshape(1, d_model), w_in_place, w_out_part, *tables)
+    )(hidden.reshape(tokens, d_model), gain, w_in_rows, w_out_part, *tables)
     return out.reshape(hidden.shape), k_rot.reshape(batch, tokens, HEAD_DIM), value.reshape(batch, tokens, HEAD_DIM)
 
 
@@ -424,20 +448,13 @@
         out_rows = w_out_local.shape[1] * group
         ff_dim = in_part * group - out_rows - 2 * HEAD_DIM
         num_heads = (out_rows - ff_dim) // HEAD_DIM
-        chip_cols = CORES * in_part
-        phases = max((chip_cols * c) % LANES for c in range(ring * ring))
-        padded = -(-(chip_cols + phases) // LANES) * LANES
-        me = lax.axis_index("fsdp")
-        offset = lax.rem(chip_cols * (me // CORES), LANES) + in_part * lax.rem(me, CORES)
+        w_in_rows = jnp.swapaxes(w_in_local, 1, 2)
         hidden = x_local
         tables = rope_tables(x_local.shape[1])
         key_list = []
         value_list = []
         for layer in range(layers):
-            w_in_place = lax.dynamic_update_slice(jnp.zeros((d_model, padded), w_in_local.dtype), w_in_local[layer],
-                                                  (0, offset))
-            hidden, k_rot, value = parallel_layer(hidden, gain[layer], w_in_place, w_out_local[layer], tables, ring,
-                                                  num_heads)
+            hidden, k_rot, value = parallel_layer(hidden, gain, w_in_rows, w_out_local, tables, ring, num_heads, layer)
             key_list.append(k_rot)
             value_list.append(value)
         return hidden, jnp.stack(key_list), jnp.stack(value_list)

time: 340 us -> 264 us (0.78)
  local copies, waits for them, and re-layouts: 69.7 us -> 1.68 us
  Pallas kernels: 266 us -> 260 us
    dynamic_update_slice x2 -> x0, local copies, waits for them, and re-layouts: 47 us -> none  [device_program(): lax.dynamic_update_slice(jnp.zeros((d_model, padded), w_in_local.dtype),...]
    unnamed x9 -> x5, local copies, waits for them, and re-layouts: 7.87 us -> 1.68 us
    slice x2 -> x0, local copies, waits for them, and re-layouts: 5.96 us -> none  [the longest x1 5.34 us: device_program(): w_in_local[layer]]
    pallas_call x2, Pallas kernels: 266 us -> 260 us  [parallel_layer(): pl.pallas_call(functools.partial(layer_kernel, ring, num_heads, layer), o...]
    another operation x2 -> x0, local copies, waits for them, and re-layouts: 5.27 us -> none
    squeeze x1 -> x0, local copies, waits for them, and re-layouts: 3.61 us -> none  [device_program(): w_out_local[layer]]
where the time goes in v3:
time: 264 us
  Pallas kernels  260 us (98%)
    pallas_call x2, Pallas kernels, parallel_layer(): pl.pallas_call(functools.partial(layer_kernel, ring, num_heads, layer), o...  260 us

profile of v3, /device:TPU:96, one launch (start us, length us, event | category | flops | bytes accessed | tf_op | source)
XLA Modules:
  0.0 263.8 jit_solution(10476723808432643711)
XLA Ops:
  0.6 134.8 %layer.2 = (bf16[64,2048]{1,0:T(8,128)(2,1)}, bf16[64,256]{1,0:T(8,128)(2,1)}, bf16[64,256]{1,0:T(8,128)(2,1)}) custom-call(bf16[64,2048]{1,0:T(8,128)(2,1)} %bitcast.9, bf16[2,2048]{1,0:T(2,128)(2,1)} %gain_ref.3, bf16[2,592,2048]{2,1,0:T(8,128)(2,1)} %bitcast.7, bf16[2,320,2048]{2,1,0:T(8,128)(2,1)} %w_out_ref.3, f32[64,128]{1,0:T(8,128)} %constant.4.clone.cos_ref, ...), custom_call_target="tpu_custom_call" | custom-call | tf_op jit(solution)/shard_map/layer/pallas_call | solution.py:402
  135.4 0.0 copy-start
  135.4 0.0 copy-start.1
  135.4 125.3 %layer.3 = (bf16[64,2048]{1,0:T(8,128)(2,1)}, bf16[64,256]{1,0:T(8,128)(2,1)}, bf16[64,256]{1,0:T(8,128)(2,1)}) custom-call(bf16[64,2048]{1,0:T(8,128)(2,1)} %get-tuple-element.9.x_ref, bf16[2,2048]{1,0:T(2,128)(2,1)} %gain_ref.3, bf16[2,592,2048]{2,1,0:T(8,128)(2,1)} %bitcast.8, bf16[2,320,2048]{2,1,0:T(8,128)(2,1)} %w_out_ref.3, ...), custom_call_target="tpu_custom_call" | custom-call | tf_op jit(solution)/shard_map/layer/pallas_call | solution.py:402
  260.7 0.0 copy-done
  260.7 0.0 copy-done.1
  260.7 1.4 pad_maximum_fusion
  262.2 1.7 copy.10
Async XLA Ops:
  135.4 125.3 %copy-start = (bf16[64,256]{1,0:T(8,128)(2,1)S(1)}, bf16[64,256]{1,0:T(8,128)(2,1)}, u32[]{:S(2)}) copy-start(bf16[64,256]{1,0:T(8,128)(2,1)} %get-tuple-element.11) | copy-start | bytes 98308
  135.4 125.3 %copy-start.1 = (bf16[64,256]{1,0:T(8,128)(2,1)S(1)}, bf16[64,256]{1,0:T(8,128)(2,1)}, u32[]{:S(2)}) copy-start(bf16[64,256]{1,0:T(8,128)(2,1)} %get-tuple-element.13) | copy-start | bytes 98308

commit v4 on v0

v4 whole, which is shorter than its diff:
```python
import functools
import math

import jax
import jax.numpy as jnp
from jax import lax
from jax.experimental import pallas as pl
from jax.experimental.pallas import tpu as pltpu
import numpy as np
from jax.sharding import PartitionSpec as P

HEAD_DIM = 256
ROPE_BASE = 10000.0
NORM_EPS = 1e-6
LANES = 128
CORES = 2
MESH = pl.DeviceIdType.MESH


def rope_tables(seq_len):
    half_dim = HEAD_DIM // 2
    inv_freq = np.float32(ROPE_BASE) ** (-np.arange(half_dim, dtype=np.float32) / np.float32(half_dim))
    angle = np.arange(seq_len, dtype=np.float32)[:, None] * inv_freq[None, :].astype(np.float32)
    return jnp.asarray(np.cos(angle), jnp.float32), jnp.asarray(np.sin(angle), jnp.float32)


GATHER, SEND_P, SEND_M, REDUCE, WEIGHT = 0, 40, 56, 72, 96
EVENTS = 98


def layers_kernel(ring, num_heads, x_ref, gain_ref, w_in_ref, w_out_ref, cos_ref, sin_ref, y_ref, k_ref, v_ref,
                 h_all, p_out, p_in, mixed_out, mixed_in, part_y, part_x,
                 opp_lo, opp_hi, ring_lo, ring_hi, last_opp_lo, last_opp_hi, last_lo, last_hi,
                 send_sem, recv_sem, local_sem, *weights):
    tokens, d_model = x_ref.shape
    half, quarter = tokens // 2, tokens // 4
    d_half = d_model // 2
    in_part = w_in_ref.shape[1]
    out_part = w_out_ref.shape[1]
    chip_rows = CORES * out_part
    real_cols = CORES * in_part
    layers = len(weights) // 2
    w_in_all, w_out_all = weights[:layers], weights[layers:]
    chip_cols = w_in_all[0].shape[0]
    me = lax.axis_index("fsdp")
    core = lax.rem(me, CORES)
    chip = me // CORES
    x = lax.rem(chip, ring)
    y = chip // ring

    def wrap(a):
        return lax.rem(a + ring, ring)

    def device(cx, cy):
        return (wrap(cy) * ring + wrap(cx)) * CORES + core

    margin = chip_cols - real_cols
    if margin:
        for buf in w_in_all:
            buf[0:margin] = jnp.zeros((margin, d_model), buf.dtype)
            buf[real_cols:chip_cols] = jnp.zeros((margin, d_model), buf.dtype)

    peer = chip * CORES + (1 - core)
    barrier = pltpu.get_barrier_semaphore()
    pl.semaphore_signal(barrier, inc=1, device_id={"fsdp": peer}, device_id_type=MESH)
    others = [(dx, dy) for dy in range(ring) for dx in range(ring) if dx or dy]
    for dx, dy in others:
        pl.semaphore_signal(barrier, inc=1, device_id={"fsdp": device(x + dx, y + dy)}, device_id_type=MESH)

    phase = lax.rem(real_cols * chip, LANES)

    def in_rows(layer, which):
        return w_in_all[layer].at[pl.ds(pl.multiple_of(phase + which * in_part, 16), in_part)]

    def out_rows(layer, which):
        return w_out_all[layer].at[pl.ds(pl.multiple_of(which * out_part, 16), out_part)]

    local = []
    for layer in range(layers):
        local.append(pltpu.make_async_copy(w_in_ref.at[layer], in_rows(layer, core), local_sem.at[2 * layer]))
        local.append(pltpu.make_async_copy(w_out_ref.at[layer], out_rows(layer, core), local_sem.at[2 * layer + 1]))
    for copy in local:
        copy.start()

    def run_layer(layer):
        first = EVENTS * layer
        source = x_ref if layer == 0 else y_ref
        sends = []
        gathers = []
        done = set()

        def send(event, src, dst, target):
            copy = pltpu.make_async_remote_copy(src_ref=src, dst_ref=dst, send_sem=send_sem.at[first + event],
                                                recv_sem=recv_sem.at[first + event], device_id={"fsdp": target},
                                                device_id_type=MESH)
            copy.start()
            (gathers if event < SEND_P else sends).append(copy)

        def need(event, dst):
            if event in done:
                return
            done.add(event)
            pltpu.make_async_remote_copy(src_ref=dst, dst_ref=dst, send_sem=send_sem.at[first + event],
                                         recv_sem=recv_sem.at[first + event], device_id={"fsdp": me},
                                         device_id_type=MESH).wait_recv()

        def send_weights(which):
            shift = EVENTS * (which - layer)
            send(shift + WEIGHT, w_in_ref.at[which], in_rows(which, core), peer)
            send(shift + WEIGHT + 1, w_out_ref.at[which], out_rows(which, core), peer)

        x_float = source[...].astype(jnp.float32)
        centred = x_float - jnp.mean(x_float, axis=-1, keepdims=True)
        variance = jnp.mean(centred * centred, axis=-1, keepdims=True)
        normed = centred * lax.rsqrt(variance + NORM_EPS) * gain_ref[layer:layer + 1].astype(jnp.float32)
        h_all[y, x] = normed.astype(jnp.bfloat16)

        if layer == 0:
            pl.semaphore_wait(barrier, len(others) + 1)

        def place(part, prim, sec):
            return (x + prim, y + sec) if part == 0 else (x + sec, y + prim)

        def block(part, prim, sec, low, count):
            cx, cy = place(part, prim, sec)
            return h_all.at[wrap(cy), wrap(cx), pl.ds(part * half + low, count)]

        def gather_send(event, part, blk, prim, sec):
            send(event, blk, blk, device(*place(part, prim, sec)))

        steps = (0, -1, 1, 2)

        def base(part):
            return GATHER + 20 * part

        def to_second(part, j):
            e = base(part) + 4 + 4 * j
            blk = block(part, steps[j], 0, 0, half)
            gather_send(e, part, blk, 0, 1)
            gather_send(e + 1, part, blk, 0, -1)

        def got_first(part, which):
            e = base(part)
            if which == -1:
                need(e, block(part, -1, 0, 0, half))
            elif which == 1:
                need(e + 1, block(part, 1, 0, 0, half))
            else:
                need(e + 2, block(part, 2, 0, 0, quarter))
                need(e + 3, block(part, 2, 0, quarter, quarter))

        def got_second(part, j, which):
            e = base(part) + 4 + 4 * j
            dp = steps[j]
            if which == -1:
                need(e, block(part, dp, -1, 0, half))
            elif which == 1:
                need(e + 1, block(part, dp, 1, 0, half))
            else:
                need(e + 2, block(part, dp, 2, 0, quarter))
                need(e + 3, block(part, dp, 2, quarter, quarter))

        def pass_second(part, j):
            e = base(part) + 4 + 4 * j
            dp = steps[j]
            got_second(part, j, -1)
            gather_send(e + 2, part, block(part, dp, -1, 0, quarter), 0, 1)
            got_second(part, j, 1)
            gather_send(e + 3, part, block(part, dp, 1, quarter, quarter), 0, -1)

        for part in (0, 1):
            own = block(part, 0, 0, 0, half)
            gather_send(base(part), part, own, 1, 0)
            gather_send(base(part) + 1, part, own, -1, 0)
        for part in (0, 1):
            to_second(part, 0)
        if layer == 0:
            send_weights(0)
        for part in (0, 1):
            got_first(part, -1)
            gather_send(base(part) + 2, part, block(part, -1, 0, 0, quarter), 1, 0)
            got_first(part, 1)
            gather_send(base(part) + 3, part, block(part, 1, 0, quarter, quarter), -1, 0)
        for part in (0, 1):
            to_second(part, 1)
            to_second(part, 2)
        for part in (0, 1):
            pass_second(part, 0)
        for part in (0, 1):
            got_first(part, 2)
            to_second(part, 3)

        local[2 * layer].wait()
        need(WEIGHT, in_rows(layer, 1 - core))

        wide = math.gcd(chip_cols, 256)

        def row_product(dy):
            row = wrap(y + dy)
            lhs = h_all[row].reshape(ring * tokens, d_model)

            @pl.loop(0, chip_cols // wide)
            def _(n):
                cols = pl.ds(pl.multiple_of(n * wide, wide), wide)
                res = lax.dot_general(lhs, w_in_all[layer][cols], (((1,), (1,)), ((), ())), preferred_element_type=jnp.float32)
                p_out[row, :, :, cols] = res.astype(jnp.bfloat16).reshape(ring, tokens, wide)

        def row_send(dy):
            row = wrap(y + dy)
            for dx in (2, 1, 3, 0):
                col = wrap(x + dx)
                if dx == 0 and dy == 0:
                    p_in[y, x] = p_out[y, x]
                else:
                    send(SEND_P + (dy % ring) * ring + dx, p_out.at[row, col], p_in.at[y, x], device(x + dx, y + dy))

        for which in (-1, 1, 2):
            got_second(1, 0, which)
        row_product(0)
        for j in (1, 2):
            for part in (0, 1):
                pass_second(part, j)
        for part in (0, 1):
            pass_second(part, 3)
        row_send(0)
        for dy, j in ((-1, 1), (1, 2), (2, 3)):
            for i in range(ring):
                got_second(0, i, dy)
            for which in (-1, 1, 2):
                got_second(1, j, which)
            row_product(dy)
            row_send(dy)

        for dx, dy in others:
            need(SEND_P + dy * ring + dx, p_in.at[wrap(y - dy), wrap(x - dx)])
        if layer + 1 < layers:
            send_weights(layer + 1)

        def tile(t):
            pieces = []
            for c in range(ring * ring):
                if c * real_cols < (t + 1) * LANES and (c + 1) * real_cols > t * LANES:
                    low = (t - (c * real_cols) // LANES) * LANES
                    pieces.append(p_in[c // ring, c % ring, :, low:low + LANES])
            return sum(pieces[1:], pieces[0])

        cos_table = cos_ref[...]
        sin_table = sin_ref[...]

        def rotated(t, scale):
            first = tile(t).astype(jnp.float32)
            second = tile(t + 1).astype(jnp.float32)
            a = first * cos_table - second * sin_table
            b = second * cos_table + first * sin_table
            return jnp.concatenate([(a * scale).astype(jnp.bfloat16), (b * scale).astype(jnp.bfloat16)], axis=-1)

        head_tiles = HEAD_DIM // LANES
        q_tiles = num_heads * head_tiles
        out_tiles = chip_rows // LANES

        def put(t, val):
            c, i = divmod(t, out_tiles)
            mixed_out[c, :, i * LANES:(i + 1) * LANES] = val

        ff_tiles = ring * ring * out_tiles - q_tiles
        for t in range(ff_tiles):
            gate = tile(q_tiles + 4 + t).astype(jnp.float32)
            up = tile(q_tiles + 4 + ff_tiles + t).astype(jnp.float32)
            put(q_tiles + t, (jax.nn.silu(gate) * up).astype(jnp.bfloat16))

        far_first = sorted(others, key=lambda d: -((d[0] == 2) + (d[1] == 2)))
        first_plain = -(-q_tiles // out_tiles)

        def mixed_send(plain):
            for dx, dy in far_first:
                dest = wrap(y + dy) * ring + wrap(x + dx)
                copy = pltpu.make_async_remote_copy(
                    src_ref=mixed_out.at[dest], dst_ref=mixed_in.at[y, x], send_sem=send_sem.at[first + SEND_M + dy * ring + dx],
                    recv_sem=recv_sem.at[first + SEND_M + dy * ring + dx], device_id={"fsdp": device(x + dx, y + dy)},
                    device_id_type=MESH)

                @pl.when(dest >= first_plain if plain else dest < first_plain)
                def _():
                    copy.start()

                if not plain:
                    sends.append(copy)

        for copy in gathers:
            copy.wait_send()
        mixed_send(True)
        query = jnp.concatenate([rotated(h * head_tiles, HEAD_DIM ** -0.5) for h in range(num_heads)], axis=0)
        key = rotated(q_tiles, 1.0)
        value = jnp.concatenate([tile(q_tiles + 2), tile(q_tiles + 3)], axis=-1)
        k_ref[layer] = key
        v_ref[layer] = value
        scores = lax.dot_general(query, key, (((1,), (1,)), ((), ())), preferred_element_type=jnp.float32)
        scores = scores.reshape(num_heads, tokens, tokens)
        q_pos = lax.broadcasted_iota(jnp.int32, scores.shape, 1)
        k_pos = lax.broadcasted_iota(jnp.int32, scores.shape, 2)
        scores = jnp.where(q_pos >= k_pos, scores, -1e30)
        weight = jnp.exp(scores - jnp.max(scores, axis=-1, keepdims=True))
        row_sum = jnp.sum(weight, axis=-1, keepdims=True)
        attended = jnp.dot(weight.astype(jnp.bfloat16).reshape(num_heads * tokens, tokens), value,
                           preferred_element_type=jnp.float32).reshape(num_heads, tokens, HEAD_DIM)
        attended = (attended / row_sum).astype(jnp.bfloat16)
        for h in range(num_heads):
            for i in range(head_tiles):
                put(h * head_tiles + i, attended[h, :, i * LANES:(i + 1) * LANES])
        mixed_send(False)
        mixed_in[y, x] = mixed_out[chip]
        local[2 * layer + 1].wait()
        need(WEIGHT + 1, out_rows(layer, 1 - core))

        parts = (part_y, part_x)
        centre = ((y, x), (x, y))

        def lined(f, prim, sec):
            return (x + sec, y + prim) if f == 0 else (x + prim, y + sec)

        def arrived(f, prim):
            for sec in range(ring):
                dx, dy = (-sec, -prim) if f == 0 else (-prim, -sec)
                dx, dy = dx % ring, dy % ring
                if dx or dy:
                    need(SEND_M + dy * ring + dx, mixed_in.at[wrap(y - dy), wrap(x - dx)])

        narrow = min(d_half, 256)

        def product(f, prim):
            arrived(f, prim)
            idx = wrap(centre[f][0] + prim)
            lhs = mixed_in[idx] if f == 0 else mixed_in[:, idx]
            lhs = lhs.reshape(ring * tokens, chip_rows)

            @pl.loop(0, d_half // narrow)
            def _(n):
                src = pl.ds(pl.multiple_of(f * d_half + n * narrow, narrow), narrow)
                cols = pl.ds(pl.multiple_of(n * narrow, narrow), narrow)
                res = jnp.dot(lhs, w_out_all[layer][:, src], preferred_element_type=jnp.float32)
                parts[f][idx, :, :, cols] = res.reshape(ring, tokens, narrow)

        lo, hi = pl.ds(0, ring // 2), pl.ds(ring // 2, ring // 2)
        t_lo, t_hi = pl.ds(0, half), pl.ds(half, half)

        def event(f, i):
            return REDUCE + 12 * f + i

        def at(f, prim):
            return wrap(centre[f][0] + prim)

        def toward(f, prim, sec):
            return device(*lined(f, prim, sec))

        for f in (0, 1):
            product(f, 2)
            send(event(f, 0), parts[f].at[at(f, 2), lo], opp_lo.at[f], toward(f, 1, 0))
            send(event(f, 1), parts[f].at[at(f, 2), hi], opp_hi.at[f], toward(f, -1, 0))
        for f in (0, 1):
            product(f, 1)
            send(event(f, 2), parts[f].at[at(f, 1), hi], ring_lo.at[f, hi], toward(f, 1, 0))
            product(f, -1)
            send(event(f, 3), parts[f].at[at(f, -1), lo], ring_hi.at[f, lo], toward(f, -1, 0))
        for f in (0, 1):
            product(f, 0)
        for f in (0, 1):
            need(event(f, 0), opp_lo.at[f])
            parts[f][at(f, 1), lo] = parts[f][at(f, 1), lo] + opp_lo[f]
            send(event(f, 4), parts[f].at[at(f, 1), lo], ring_lo.at[f, lo], toward(f, 1, 0))
            need(event(f, 1), opp_hi.at[f])
            parts[f][at(f, -1), hi] = parts[f][at(f, -1), hi] + opp_hi[f]
            send(event(f, 5), parts[f].at[at(f, -1), hi], ring_hi.at[f, hi], toward(f, -1, 0))

        def second(f, sec):
            return wrap(centre[f][1] + sec)

        for f in (0, 1):
            need(event(f, 2), ring_lo.at[f, hi])
            need(event(f, 3), ring_hi.at[f, lo])
            need(event(f, 4), ring_lo.at[f, lo])
            need(event(f, 5), ring_hi.at[f, hi])
            mid = at(f, 0)
            parts[f][mid] = parts[f][mid] + ring_lo[f] + ring_hi[f]
            send(event(f, 6), parts[f].at[mid, second(f, 2), t_lo], last_opp_lo.at[f], toward(f, 0, 1))
            send(event(f, 7), parts[f].at[mid, second(f, 2), t_hi], last_opp_hi.at[f], toward(f, 0, -1))
            send(event(f, 8), parts[f].at[mid, second(f, 1), t_hi], last_lo.at[f, t_hi], toward(f, 0, 1))
            send(event(f, 9), parts[f].at[mid, second(f, -1), t_lo], last_hi.at[f, t_lo], toward(f, 0, -1))
        for f in (0, 1):
            mid = at(f, 0)
            need(event(f, 6), last_opp_lo.at[f])
            parts[f][mid, second(f, 1), t_lo] = parts[f][mid, second(f, 1), t_lo] + last_opp_lo[f]
            send(event(f, 10), parts[f].at[mid, second(f, 1), t_lo], last_lo.at[f, t_lo], toward(f, 0, 1))
            need(event(f, 7), last_opp_hi.at[f])
            parts[f][mid, second(f, -1), t_hi] = parts[f][mid, second(f, -1), t_hi] + last_opp_hi[f]
            send(event(f, 11), parts[f].at[mid, second(f, -1), t_hi], last_hi.at[f, t_hi], toward(f, 0, -1))
        for f in (0, 1):
            need(event(f, 8), last_lo.at[f, t_hi])
            need(event(f, 9), last_hi.at[f, t_lo])
            need(event(f, 10), last_lo.at[f, t_lo])
            need(event(f, 11), last_hi.at[f, t_hi])
            out_sum = parts[f][at(f, 0), second(f, 0)] + last_lo[f] + last_hi[f]
            cols = slice(f * d_half, (f + 1) * d_half)
            y_ref[:, cols] = (source[:, cols].astype(jnp.float32) + out_sum).astype(jnp.bfloat16)
        for copy in sends:
            copy.wait_send()

    for layer in range(layers):
        run_layer(layer)


def parallel_layers(hidden, gain, w_in_rows, w_out_part, tables, ring, num_heads):
    batch, tokens, d_model = hidden.shape
    layers, out_part, _ = w_out_part.shape
    real_cols = CORES * w_in_rows.shape[1]
    margin = max((real_cols * c) % LANES for c in range(ring * ring))
    padded_cols = -(-(real_cols + margin) // LANES) * LANES
    chip_rows = CORES * out_part
    d_half = d_model // 2
    bf16, f32 = jnp.bfloat16, jnp.float32
    vmem = pl.BlockSpec(memory_space=pltpu.VMEM)
    anywhere = pl.BlockSpec(memory_space=pl.ANY)
    out, k_rot, value = pl.pallas_call(
        functools.partial(layers_kernel, ring, num_heads),
        out_shape=(
            jax.ShapeDtypeStruct((tokens, d_model), bf16),
            jax.ShapeDtypeStruct((layers, tokens, HEAD_DIM), bf16),
            jax.ShapeDtypeStruct((layers, tokens, HEAD_DIM), bf16),
        ),
        in_specs=[vmem, vmem, anywhere, anywhere, vmem, vmem],
        out_specs=(vmem, vmem, vmem),
        scratch_shapes=[
            pltpu.VMEM((ring, ring, tokens, d_model), bf16),
            pltpu.VMEM((ring, ring, tokens, padded_cols), bf16),
            pltpu.VMEM((ring, ring, tokens, padded_cols), bf16),
            pltpu.VMEM((ring * ring, tokens, chip_rows), bf16),
            pltpu.VMEM((ring, ring, tokens, chip_rows), bf16),
            pltpu.VMEM((ring, ring, tokens, d_half), f32),
            pltpu.VMEM((ring, ring, tokens, d_half), f32),
            pltpu.VMEM((2, ring // 2, tokens, d_half), f32),
            pltpu.VMEM((2, ring // 2, tokens, d_half), f32),
            pltpu.VMEM((2, ring, tokens, d_half), f32),
            pltpu.VMEM((2, ring, tokens, d_half), f32),
            pltpu.VMEM((2, tokens // 2, d_half), f32),
            pltpu.VMEM((2, tokens // 2, d_half), f32),
            pltpu.VMEM((2, tokens, d_half), f32),
            pltpu.VMEM((2, tokens, d_half), f32),
            pltpu.SemaphoreType.DMA((layers * EVENTS,)),
            pltpu.SemaphoreType.DMA((layers * EVENTS,)),
            pltpu.SemaphoreType.DMA((2 * layers,)),
        ] + [pltpu.VMEM((padded_cols, d_model), bf16)] * layers + [pltpu.VMEM((chip_rows, d_model), bf16)] * layers,
        compiler_params=pltpu.CompilerParams(collective_id=0, has_side_effects=True, vmem_limit_bytes=62 * 2 ** 20),
        name="layers",
    )(hidden.reshape(tokens, d_model), gain, w_in_rows, w_out_part, *tables)
    caches = (layers, batch, tokens, HEAD_DIM)
    return out.reshape(hidden.shape), k_rot.reshape(caches), value.reshape(caches)


def solution(mesh):
    batch_axes = ("dp", "fsdp")
    group = mesh.shape["fsdp"]
    ring = math.isqrt(group // CORES)
    if ring != 4 or ring * ring * CORES != group:
        raise ValueError("unsupported group")

    def device_program(x_local, gain, w_in_local, w_out_local):
        layers, d_model, in_part = w_in_local.shape
        out_rows = w_out_local.shape[1] * group
        ff_dim = in_part * group - out_rows - 2 * HEAD_DIM
        num_heads = (out_rows - ff_dim) // HEAD_DIM
        w_in_rows = jnp.swapaxes(w_in_local, 1, 2)
        tables = rope_tables(x_local.shape[1])
        return parallel_layers(x_local, gain, w_in_rows, w_out_local, tables, ring, num_heads)

    return jax.shard_map(
        device_program,
        mesh=mesh,
        in_specs=(P(batch_axes, None, None), P(None, None), P(None, None, "fsdp"), P(None, "fsdp", None)),
        out_specs=(P(batch_axes, None, None), P(None, batch_axes, None, None), P(None, batch_axes, None, None)),
        check_vma=False,
    )
```

time: 754 us -> 260 us (0.34)
  waiting for transfers between devices: 625 us -> 0 us
  Pallas kernels: 0 us -> 254 us
  matrix products: 102 us -> 0 us
  between operations: 14 us -> 0.64 us
    all_gather x4 -> x0, waiting for transfers between devices: 623 us -> none  [the longest x2 427 us: device_program(): w_in_full = lax.all_gather(w_in_local[layer], 'fsdp', axis=1, tiled=True)]
    pallas_call x0 -> x1, Pallas kernels: none -> 254 us  [parallel_layers(): pl.pallas_call(functools.partial(layers_kernel, ring, num_heads), out_sha...]
    dot_general x10 -> x0, matrix products: 102 us -> none  [the longest x2 62.4 us: parallel_layer(): jnp.einsum('bsd,de->bse', normed, w_in_full, preferred_element_type=jnp.f...]
  transfers between devices with their start and end apart: 4 -> 0, of which waited for: 4 -> 0; matrix products, arithmetic and copies ran while one was open for 12% -> 0% of each run, Pallas kernels for 0% -> 0%
where the time goes in v4:
time: 260 us
  Pallas kernels  254 us (98%)
  local copies, waits for them, and re-layouts  4.61 us (2%)
    pallas_call x1, Pallas kernels, parallel_layers(): pl.pallas_call(functools.partial(layers_kernel, ring, num_heads), out_sha...  254 us

profile of v4, /device:TPU:96, one launch (start us, length us, event | category | flops | bytes accessed | tf_op | source)
XLA Modules:
  0.0 259.6 jit_solution(4544868910749301320)
XLA Ops:
  0.6 254.3 %layers.1 = (bf16[64,2048]{1,0:T(8,128)(2,1)}, bf16[2,64,256]{2,1,0:T(8,128)(2,1)}, bf16[2,64,256]{2,1,0:T(8,128)(2,1)}) custom-call(bf16[64,2048]{1,0:T(8,128)(2,1)} %bitcast.10, bf16[2,2048]{1,0:T(2,128)(2,1)} %gain_ref.1, bf16[2,592,2048]{2,1,0:T(8,128)(2,1)} %bitcast.9, bf16[2,320,2048]{2,1,0:T(8,128)(2,1)} %w_out_ref.1, ...), custom_call_target="tpu_custom_call" | custom-call | tf_op jit(solution)/shard_map/layers/pallas_call | solution.py:422
  255.0 1.7 copy.14
  256.6 1.5 copy.15
  258.1 1.5 copy.16
